TPU v7x, 32 devices: a whole 2x2x4 slice. The times are simulated.
32 devices in a mesh: dp: 8 (over y, x, core), expert: 4 (over z).
Axes of the slice: x: 2, y: 2, z: 4, core: 2. Of those that a mesh axis runs over, the one named last changes fastest.
Arguments:
- tokens: bfloat16 [4096, 2048], P(('dp', 'expert')), may hold values from -6 to 6
- cotangent: bfloat16 [4096, 2048], P(('dp', 'expert')), may hold values from -6 to 6
- expert_ids: int32 [4096, 2], P(('dp', 'expert')), may hold values from 0 to 3, all different within a row; in each aligned block of 128 rows (0 to 127, 128 to 255, ...) at most 128 rows name the same one
- combine: float32 [4096, 2], P(('dp', 'expert')), may hold values from 0.1 to 1
- w_gate: bfloat16 [4, 2048, 768], P('expert'), may hold values from -0.125 to 0.125
- w_up: bfloat16 [4, 2048, 768], P('expert'), may hold values from -0.125 to 0.125
- w_down: bfloat16 [4, 768, 2048], P('expert'), may hold values from -0.21875 to 0.21875
Outputs:
- input_grad: bfloat16 [4096, 2048], P(('dp', 'expert'))
- combine_grad: float32 [4096, 2], P(('dp', 'expert'))
- gate_grad: bfloat16 [4, 2048, 768], P('expert', 'dp')
- up_grad: bfloat16 [4, 2048, 768], P('expert', 'dp')
- down_grad: bfloat16 [4, 768, 2048], P('expert', 'dp')
Inputs may be any that keep to these rules, and one draw needn't show every extreme that they name: `expert_ids`: each token names 2 different experts. In the rows of one device no expert is named by more than 128 tokens, and in some devices' rows some expert is named by exactly 128.
All inputs are finite; a program needn't handle non-finite values.
Results may differ from a plain program's by a relative error of at most 0.02.
Values may be sent and summed in bfloat16 or wider, within the bound.
A program may use at most 128 MiB of HBM per device.

v0:
```python
import functools
import jax
import jax.numpy as jnp
from jax import lax
from jax.experimental import pallas as pl
from jax.experimental.pallas import tpu as pltpu
from jax.sharding import PartitionSpec as P

MESH = pl.DeviceIdType.MESH
VMEM = pl.BlockSpec(memory_space=pltpu.VMEM)
LIMIT = 56 * 1024 * 1024


def remote(src, dst, send, recv, axis, target):
    return pltpu.make_async_remote_copy(
        src_ref=src,
        dst_ref=dst,
        send_sem=send,
        recv_sem=recv,
        device_id={axis: target},
        device_id_type=MESH,
    )


def gather_kernel(n, x, dy, w, x_all, dy_all, w_all, send, recv, w_send, w_recv):
    me = lax.axis_index("expert")
    barrier = pltpu.get_barrier_semaphore()
    for k in range(1, n):
        pl.semaphore_signal(
            barrier, inc=1, device_id={"expert": lax.rem(me + k, n)}, device_id_type=MESH
        )
    pl.semaphore_wait(barrier, n - 1)

    def hop(t, side, s):
        own, full = ((x, x_all), (dy, dy_all))[t]
        step = 1 if side == 0 else -1
        block = jnp.clip(me - step * s, 0, n - 1)
        src = own if s == 0 else full.at[block]
        target = jnp.clip(me + step, 0, n - 1)
        return remote(
            src, full.at[block], send.at[t, side, s], recv.at[t, side, s], "expert", target
        )

    def arrival(t, side, s):
        full = (x_all, dy_all)[t]
        step = 1 if side == 0 else -1
        block = jnp.clip(me - step * (s + 1), 0, n - 1)
        slot = full.at[block]
        return remote(slot, slot, send.at[t, side, s], recv.at[t, side, s], "expert", me)

    def sends(side, s):
        if side == 0:
            return jnp.logical_and(me >= s, me + 1 < n)
        return jnp.logical_and(me + s < n, me >= 1)

    def gets(side, s):
        return me >= s + 1 if side == 0 else me + s + 1 < n

    for t in range(2):
        for s in range(n):
            for side in range(2):
                if s >= 1:

                    @pl.when(gets(side, s - 1))
                    def _():
                        arrival(t, side, s - 1).wait_recv()

                if s < n - 1:

                    @pl.when(sends(side, s))
                    def _():
                        hop(t, side, s).start()

            if s == 0:
                if t == 0:
                    small = []
                    for k in range(1, n):
                        small.append(
                            remote(
                                w,
                                w_all.at[k],
                                w_send.at[k],
                                w_recv.at[k],
                                "expert",
                                lax.rem(me + k, n),
                            )
                        )
                        small[-1].start()
                    x_all[me] = x[...]
                    dy_all[me] = dy[...]
                    w_all[0] = w[...]
    for t in range(2):
        for s in range(n - 1):
            for side in range(2):

                @pl.when(sends(side, s))
                def _():
                    hop(t, side, s).wait_send()

    for copy in small:
        copy.wait()


def gather_all(n, x, dy, w):
    outs = [jax.ShapeDtypeStruct((n,) + a.shape, a.dtype) for a in (x, dy, w)]
    return pl.pallas_call(
        functools.partial(gather_kernel, n),
        out_shape=outs,
        in_specs=[VMEM] * 3,
        out_specs=[VMEM] * 3,
        scratch_shapes=[
            pltpu.SemaphoreType.DMA((2, 2, n)),
            pltpu.SemaphoreType.DMA((2, 2, n)),
            pltpu.SemaphoreType.DMA((n,)),
            pltpu.SemaphoreType.DMA((n,)),
        ],
        compiler_params=pltpu.CompilerParams(
            collective_id=0, has_side_effects=True, vmem_limit_bytes=LIMIT
        ),
        name="gather_all",
    )(x, dy, w)


def reduce_kernel(n, bits, *refs):
    rows, comb, both, down, in_grad, comb_all, gate_out, up_out, down_out = refs[:9]
    got_rows, r_send, r_recv, c_send, c_recv = refs[9:14]
    rest = refs[14:]
    gots = [rest[2 * p : 2 * p + 2] for p in range(bits)]
    sums = [rest[2 * bits + 2 * p : 2 * bits + 2 * p + 2] for p in range(bits - 1)]
    send, recv = rest[-2:]
    me = lax.axis_index("expert")
    rank = lax.axis_index("dp")
    bit = [lax.rem(rank // (1 << b), 2) for b in range(bits)]
    mate = [rank + (1 - 2 * bit[b]) * (1 << b) for b in range(bits)]
    barrier = pltpu.get_barrier_semaphore()
    for k in range(1, n):
        pl.semaphore_signal(
            barrier, inc=1, device_id={"expert": lax.rem(me + k, n)}, device_id_type=MESH
        )
    for b in range(bits):
        pl.semaphore_signal(barrier, inc=1, device_id={"dp": mate[b]}, device_id_type=MESH)
    pl.semaphore_wait(barrier, n - 1 + bits)

    orders = ([0] + list(range(1, bits)), [0] + list(range(bits - 1, 0, -1)))
    inputs = (both, down)

    def span(a, h):
        half = inputs[a].shape[2] // 2
        return pl.ds(h * half, half)

    def block_of(order, value, m):
        block = value * (1 << order[0])
        for i, b in enumerate(order[1:]):
            block = block + lax.rem(m // (1 << i), 2) * (1 << b)
        return block

    def copy(p, h, a, m):
        order = orders[h]
        b = order[p]
        if p == 0:
            src = inputs[a].at[block_of(order, 1 - bit[b], m), :, span(a, h)]
        else:
            src = sums[p - 1][a].at[h, 1 - bit[b] + 2 * m]
        return remote(
            src, gots[p][a].at[h, m], send.at[p, h, a, m], recv.at[p, h, a, m], "dp", mate[b]
        )

    def slots(p, h):
        count = 1 << (bits - 1 - p)
        if count == 1:
            return [(0, None)]
        lead = bit[orders[h][p + 1]]
        going = [(1 - lead + 2 * k, k) for k in range(count // 2)]
        return going + [(lead + 2 * k, None) for k in range(count // 2)]

    for h in range(2):
        for m, _ in slots(0, h):
            for a in range(2):
                copy(0, h, a, m).start()
    exchange = []
    for k in range(1, n):
        target = lax.rem(me + k, n)
        exchange.append(
            remote(rows.at[target], got_rows.at[k], r_send.at[k], r_recv.at[k], "expert", target)
        )
        exchange.append(
            remote(comb.at[target], comb_all.at[k], c_send.at[k], c_recv.at[k], "expert", target)
        )
    for item in exchange:
        item.start()
    comb_all[0] = comb[me]

    for p in range(bits):
        plans = [slots(p, h) for h in range(2)]
        for i in range(len(plans[0])):
            for h in range(2):
                m, onward = plans[h][i]
                order = orders[h]
                mine = bit[order[p]]
                for a in range(2):
                    copy(p, h, a, m).wait_recv()
                    if p == 0:
                        held = inputs[a][block_of(order, mine, m), :, span(a, h)]
                    else:
                        held = sums[p - 1][a][h, mine + 2 * m]
                    total = held.astype(jnp.float32) + gots[p][a][h, m].astype(jnp.float32)
                    total = total.astype(jnp.bfloat16)
                    if p < bits - 1:
                        sums[p][a][h, m] = total
                        if onward is not None:
                            copy(p + 1, h, a, onward).start()
                    elif a == 0:
                        (gate_out, up_out)[h][...] = total
                    else:
                        down_out[:, span(a, h)] = total
    for item in exchange:
        item.wait_recv()
    summed = rows[me].astype(jnp.float32)
    for k in range(1, n):
        summed = summed + got_rows[k].astype(jnp.float32)
    in_grad[...] = summed.astype(jnp.bfloat16)
    for item in exchange:
        item.wait_send()
    for p in range(bits):
        for h in range(2):
            for m, _ in slots(p, h):
                for a in range(2):
                    copy(p, h, a, m).wait_send()


def reduce_all(n, replicas, rows, comb, both, down):
    bits = replicas.bit_length() - 1
    width = both.shape[2] // 2
    bf16 = jnp.bfloat16
    outs = [
        jax.ShapeDtypeStruct(rows.shape[1:], bf16),
        jax.ShapeDtypeStruct(comb.shape, jnp.float32),
        jax.ShapeDtypeStruct((both.shape[1], width), bf16),
        jax.ShapeDtypeStruct((both.shape[1], width), bf16),
        jax.ShapeDtypeStruct(down.shape[1:], bf16),
    ]
    halves = [(a.shape[1], a.shape[2] // 2) for a in (both, down)]
    scratch = [pltpu.VMEM(rows.shape, bf16)]
    scratch += [pltpu.SemaphoreType.DMA((n,))] * 4
    for phases in (bits, bits - 1):
        for p in range(phases):
            scratch += [pltpu.VMEM((2, 1 << (bits - 1 - p)) + half, bf16) for half in halves]
    scratch += [pltpu.SemaphoreType.DMA((bits, 2, 2, 1 << (bits - 1)))] * 2
    return pl.pallas_call(
        functools.partial(reduce_kernel, n, bits),
        out_shape=outs,
        in_specs=[VMEM] * 4,
        out_specs=[VMEM] * 5,
        scratch_shapes=scratch,
        compiler_params=pltpu.CompilerParams(
            collective_id=1, has_side_effects=True, vmem_limit_bytes=LIMIT
        ),
        name="reduce_all",
    )(rows, comb, both, down)


def shards(tokens, cotangent, expert_ids, combine, w_gate, w_up, w_down):
    first = (((0,), (0,)), ((), ()))
    last = (((1,), (1,)), ((), ()))
    groups = lax.axis_size("expert")
    replicas = lax.axis_size("dp")
    me = lax.axis_index("expert")
    rows, top = expert_ids.shape
    feature = tokens.shape[1]
    hidden_width = w_gate.shape[2]
    names = jnp.arange(groups, dtype=jnp.int32)
    hits = expert_ids[:, :, None] == names
    weight = jnp.sum(jnp.where(hits, combine[:, :, None], 0.0), axis=1)
    table = jnp.pad(weight.T, ((0, -groups % 8), (0, 0)))
    x, dy, tables = gather_all(groups, tokens, cotangent, table)
    x = x.reshape(groups * rows, feature)
    dy = dy.reshape(groups * rows, feature)
    sources = lax.rem(me - names + groups, groups)
    mine = lax.dynamic_index_in_dim(tables, me, axis=1, keepdims=False)
    coeff = mine[sources].reshape(groups * rows, 1)
    w_g, w_u, w_d = w_gate[0], w_up[0], w_down[0]
    gate = jnp.dot(x, w_g, preferred_element_type=jnp.float32)
    up = jnp.dot(x, w_u, preferred_element_type=jnp.float32)
    sig = jax.nn.sigmoid(gate)
    act = gate * sig
    hidden = (act * up).astype(jnp.bfloat16)
    scaled = (coeff * dy.astype(jnp.float32)).astype(jnp.bfloat16)
    output = jnp.dot(hidden, w_d, preferred_element_type=jnp.float32)
    comb = jnp.sum(dy.astype(jnp.float32) * output, axis=1)
    hidden_grad = lax.dot_general(scaled, w_d, last, preferred_element_type=jnp.float32)
    gate_d = (hidden_grad * up * (sig * (1.0 + gate * (1.0 - sig)))).astype(jnp.bfloat16)
    up_d = (hidden_grad * act).astype(jnp.bfloat16)
    row = lax.dot_general(gate_d, w_g, last, preferred_element_type=jnp.float32)
    row = row + lax.dot_general(up_d, w_u, last, preferred_element_type=jnp.float32)
    row = row.astype(jnp.bfloat16).reshape(groups, rows, feature)
    paired = jnp.concatenate([gate_d, up_d], axis=1)
    both = lax.dot_general(x, paired, first, preferred_element_type=jnp.float32)
    both = both.astype(jnp.bfloat16).reshape(replicas, feature // replicas, 2 * hidden_width)
    down = lax.dot_general(hidden, scaled, first, preferred_element_type=jnp.float32)
    down = down.astype(jnp.bfloat16).reshape(replicas, hidden_width // replicas, feature)
    comb = jnp.broadcast_to(comb.reshape(groups, 1, rows), (groups, 8, rows))
    input_grad, combs, gate_grad, up_grad, down_grad = reduce_all(
        groups, replicas, row, comb, both, down
    )
    comb = combs[sources, 0]
    combine_grad = jnp.sum(jnp.where(hits, comb.T[:, None, :], 0.0), axis=2)
    return (input_grad, combine_grad, gate_grad[None], up_grad[None], down_grad[None])


def solution(mesh):
    by_token = P(("dp", "expert"), None)
    by_expert = P("expert", None, None)
    by_row = P("expert", "dp", None)
    return jax.shard_map(
        shards,
        mesh=mesh,
        in_specs=(by_token,) * 4 + (by_expert,) * 3,
        out_specs=(by_token, by_token, by_row, by_row, by_row),
        check_vma=False,
    )
```

profile of v0, /device:TPU:0, one launch (start us, length us, event | category | flops | bytes accessed | tf_op | source)
XLA Modules:
  0.0 170.2 jit_solution(9103448196710936432)
XLA Ops:
  0.6 0.0 copy-start
  0.6 0.9 select_reduce_fusion.1
  1.5 0.6 pad.5.w
  2.1 78.3 %gather_all.1 = (bf16[4,128,2048]{2,1,0:T(8,128)(2,1)}, bf16[4,128,2048]{2,1,0:T(8,128)(2,1)}, f32[4,8,128]{2,1,0:T(8,128)}) custom-call(bf16[128,2048]{1,0:T(8,128)(2,1)} %x.5, bf16[128,2048]{1,0:T(8,128)(2,1)} %dy.1, f32[8,128]{1,0:T(8,128)} %pad.5.w), custom_call_target="tpu_custom_call" | custom-call | tf_op jit(solution)/shard_map/gather_all/pallas_call | solution.py:106
  80.4 5.5 %fusion.5 = f32[512,768]{1,0:T(8,128)} fusion(bf16[512,2048]{1,0:T(8,128)(2,1)} %bitcast.64, bf16[1,2048,768]{2,1,0:T(8,128)(2,1)} %param.11), kind=kOutput, calls=%fused_computation.13 | convolution fusion | flops 1610612736 | bytes 6815744 | tf_op jit(solution)/shard_map/dot_general | solution.py:282
  85.9 0.7 constant_dynamic-slice_fusion
  86.6 0.6 gather_fusion
  87.2 0.0 copy-start.6
  87.2 2.1 %fusion = bf16[4,128,2048]{2,1,0:T(8,128)(2,1)S(1)} fusion(bf16[4,128,2048]{2,1,0:T(8,128)(2,1)} %get-tuple-element.14, f32[4,128]{1,0:T(4,128)S(1)} %gather_fusion), kind=kLoop, calls=%fused_computation.6 | loop fusion | flops 3145728 | bytes 4196352 | tf_op jit(solution)/shard_map/convert_element_type | solution.py:287
  89.3 0.4 copy-done.6
  89.7 0.0 copy-start.7
  89.7 0.0 copy-start.8
  89.7 1.9 %fusion.12 = f32[512,768]{1,0:T(8,128)S(1)} fusion(bf16[512,2048]{1,0:T(8,128)(2,1)S(1)} %bitcast.54, bf16[1,768,2048]{2,1,0:T(8,128)(2,1)S(1)} %copy-done.6), kind=kOutput, calls=%fused_computation.20 | convolution fusion | flops 1610612736 | bytes 6815744 | tf_op jit(solution)/shard_map/dot_general | solution.py:290
  91.6 0.0 copy-done
  91.6 0.0 copy-done.7
  91.6 0.2 copy-done.8
  91.7 0.0 copy-start.5
  91.8 2.3 %multiply_convert_fusion = (bf16[512,768]{1,0:T(8,128)(2,1)S(1)}, bf16[512,768]{1,0:T(8,128)(2,1)S(1)}, bf16[512,768]{1,0:T(8,128)(2,1)S(1)}) fusion(f32[512,768]{1,0:T(8,128)S(1)} %copy-done.8, f32[512,768]{1,0:T(8,128)S(1)} %fusion.12, bf16[512,2048]{1,0:T(8,128)(2,1)S(1)} %bitcast.65, bf16[1,2048,768]{2,1,0:T(8,128)(2,1)S(1)} %copy-done), kind=kOutput, calls=%fused_computation.25 | convolution fusion | flops 1616510976 | bytes 10747904 | tf_op jit(solution)/shard_map/dot_general | solution.py:283
  94.0 0.0 copy-done.5
  94.0 1.8 %fusion.3 = f32[512,2048]{1,0:T(8,128)S(1)} fusion(bf16[512,768]{1,0:T(8,128)(2,1)S(1)} %get-tuple-element.22, bf16[1,2048,768]{2,1,0:T(8,128)(2,1)S(1)} %copy-done.5), kind=kOutput, calls=%fused_computation.11 | convolution fusion | flops 1610612736 | bytes 8126464 | tf_op jit(solution)/shard_map/dot_general | solution.py:293
  95.9 0.0 copy-start.1
  95.9 3.2 %add_convert_fusion = bf16[512,2048]{1,0:T(8,128)(2,1)} fusion(f32[512,2048]{1,0:T(8,128)S(1)} %fusion.3, bf16[512,768]{1,0:T(8,128)(2,1)S(1)} %get-tuple-element.23, bf16[1,2048,768]{2,1,0:T(8,128)(2,1)S(1)} %copy-done), kind=kOutput, calls=%fused_computation.9 | convolution fusion | flops 1612709888 | bytes 10223616 | tf_op jit(solution)/shard_map/dot_general | solution.py:294
  99.0 0.0 copy-done.1
  99.0 2.0 %fusion.1 = f32[512]{0:T(512)S(1)} fusion(bf16[4,128,2048]{2,1,0:T(8,128)(2,1)S(1)} %copy-done.1, bf16[512,768]{1,0:T(8,128)(2,1)S(1)} %get-tuple-element.21, bf16[1,768,2048]{2,1,0:T(8,128)(2,1)S(1)} %copy-done.6), kind=kOutput, calls=%fused_computation.7 | convolution fusion | flops 1613757952 | bytes 6031360 | tf_op jit(solution)/shard_map/dot_general | solution.py:288
  101.0 0.6 broadcast_in_dim.47.refs_1_
  101.6 5.6 %convolution_convert_fusion = bf16[2048,1536]{1,0:T(8,128)(2,1)} fusion(bf16[512,2048]{1,0:T(8,128)(2,1)S(1)} %bitcast.66, bf16[512,768]{1,0:T(8,128)(2,1)S(1)} %get-tuple-element.23, bf16[512,768]{1,0:T(8,128)(2,1)S(1)} %get-tuple-element.22), kind=kOutput, calls=%fused_computation.2 | convolution fusion | flops 3227516928 | bytes 9961472 | tf_op jit(solution)/shard_map/dot_general | solution.py:297
  107.2 0.4 fusion.2
  107.7 3.5 %convolution_convert_fusion.1 = bf16[768,2048]{1,0:T(8,128)(2,1)} fusion(bf16[512,768]{1,0:T(8,128)(2,1)S(1)} %get-tuple-element.21, bf16[512,2048]{1,0:T(8,128)(2,1)S(1)} %fusion.2), kind=kOutput, calls=%fused_computation.10 | convolution fusion | flops 1612185600 | bytes 6029312 | tf_op jit(solution)/shard_map/dot_general | solution.py:299
  111.2 0.0 copy-start.4
  111.2 51.9 %reduce_all.1 = (bf16[128,2048]{1,0:T(8,128)(2,1)}, f32[4,8,128]{2,1,0:T(8,128)}, bf16[256,768]{1,0:T(8,128)(2,1)}, bf16[256,768]{1,0:T(8,128)(2,1)}, bf16[96,2048]{1,0:T(8,128)(2,1)}) custom-call(bf16[4,128,2048]{2,1,0:T(8,128)(2,1)} %bitcast.55, f32[4,8,128]{2,1,0:T(8,128)} %broadcast_in_dim.47.refs_1_, bf16[8,256,1536]{2,1,0:T(8,128)(2,1)} %bitcast.52, ...), custom_call_target="tpu_custom_call" | custom-call | tf_op jit(solution)/shard_map/reduce_all/pallas_call | solution.py:249
  163.1 0.0 copy-start.2
  163.1 1.3 gather_fusion.1
  164.5 0.0 copy-start.3
  164.5 0.0 copy-done.4
  164.5 0.6 select_reduce_fusion
  165.1 1.9 %copy.19 = bf16[128,2048]{1,0:T(8,128)(2,1)} copy(bf16[128,2048]{1,0:T(8,128)(2,1)} %get-tuple-element.31) | data formatting | bytes 1048576
  167.0 1.8 %copy.20 = bf16[1,256,768]{2,1,0:T(8,128)(2,1)} copy(bf16[1,256,768]{2,1,0:T(8,128)(2,1)} %bitcast.58) | data formatting | bytes 786432
  168.7 0.0 copy-done.3
  168.7 0.7 copy.21
  169.5 0.0 copy-done.2
  169.5 0.7 copy.22
  (2 shorter events, 0.0 us)
Async XLA Ops:
  0.6 90.9 %copy-start = (bf16[1,2048,768]{2,1,0:T(8,128)(2,1)S(1)}, bf16[1,2048,768]{2,1,0:T(8,128)(2,1)}, u32[]{:S(2)}) copy-start(bf16[1,2048,768]{2,1,0:T(8,128)(2,1)} %param.12) | copy-start | bytes 9437188
  87.2 2.5 %copy-start.6 = (bf16[1,768,2048]{2,1,0:T(8,128)(2,1)S(1)}, bf16[1,768,2048]{2,1,0:T(8,128)(2,1)}, u32[]{:S(2)}) copy-start(bf16[1,768,2048]{2,1,0:T(8,128)(2,1)} %param.13) | copy-start | bytes 9437188
  89.7 1.9 %copy-start.7 = (bf16[4,128,2048]{2,1,0:T(8,128)(2,1)S(1)}, bf16[4,128,2048]{2,1,0:T(8,128)(2,1)}, u32[]{:S(2)}) copy-start(bf16[4,128,2048]{2,1,0:T(8,128)(2,1)} %get-tuple-element.15) | copy-start | bytes 6291460
  89.7 2.0 %copy-start.8 = (f32[512,768]{1,0:T(8,128)S(1)}, f32[512,768]{1,0:T(8,128)}, u32[]{:S(2)}) copy-start(f32[512,768]{1,0:T(8,128)} %fusion.5) | copy-start | bytes 4718596
  91.7 2.3 %copy-start.5 = (bf16[1,2048,768]{2,1,0:T(8,128)(2,1)S(1)}, bf16[1,2048,768]{2,1,0:T(8,128)(2,1)}, u32[]{:S(2)}) copy-start(bf16[1,2048,768]{2,1,0:T(8,128)(2,1)} %param.11) | copy-start | bytes 9437188
  95.9 3.2 %copy-start.1 = (bf16[4,128,2048]{2,1,0:T(8,128)(2,1)S(1)}, bf16[4,128,2048]{2,1,0:T(8,128)(2,1)}, u32[]{:S(2)}) copy-start(bf16[4,128,2048]{2,1,0:T(8,128)(2,1)} %get-tuple-element.14) | copy-start | bytes 6291460
  111.2 53.3 %copy-start.4 = (s32[128,2]{0,1:T(2,128)S(1)}, s32[128,2]{0,1:T(2,128)}, u32[]{:S(2)}) copy-start(s32[128,2]{0,1:T(2,128)} %param.9) | copy-start | bytes 3076
  163.1 6.3 %copy-start.2 = (bf16[96,2048]{1,0:T(8,128)(2,1)S(1)}, bf16[96,2048]{1,0:T(8,128)(2,1)}, u32[]{:S(2)}) copy-start(bf16[96,2048]{1,0:T(8,128)(2,1)} %get-tuple-element.20) | copy-start | bytes 1179652
  164.5 4.2 %copy-start.3 = (bf16[256,768]{1,0:T(8,128)(2,1)S(1)}, bf16[256,768]{1,0:T(8,128)(2,1)}, u32[]{:S(2)}) copy-start(bf16[256,768]{1,0:T(8,128)(2,1)} %get-tuple-element.19) | copy-start | bytes 1179652
where the time goes:
time: 171 us; the launch traced here: 170 us
  Pallas kernels  130 us (76%)
  matrix products  25.7 us (15%)
  local copies, waits for them, and re-layouts  9.52 us (6%)
  other arithmetic  4.01 us (2%)
    pallas_call x1, Pallas kernels, gather_all(): pl.pallas_call(functools.partial(gather_kernel, n), out_shape=outs, in_sp...  78.3 us
    pallas_call x1, Pallas kernels, reduce_all(): pl.pallas_call(functools.partial(reduce_kernel, n, bits), out_shape=outs,...  51.9 us
    unnamed x22, local copies, waits for them, and re-layouts  5.69 us
    dot_general x1, matrix products, shards(): both = lax.dot_general(x, paired, first, preferred_element_type=jnp.float32)  5.63 us
    dot_general x1, matrix products, shards(): gate = jnp.dot(x, w_g, preferred_element_type=jnp.float32)  5.49 us
    dot_general x1, matrix products, shards(): lax.dot_general(hidden, scaled, first, preferred_element_type=jnp.float32)  3.54 us

commit v1 on v0

v1 whole, which is shorter than its diff:
```python
import functools
import jax
import jax.numpy as jnp
from jax import lax
from jax.experimental import pallas as pl
from jax.experimental.pallas import tpu as pltpu
from jax.sharding import PartitionSpec as P

MESH = pl.DeviceIdType.MESH
VMEM = pl.BlockSpec(memory_space=pltpu.VMEM)
HBM = pl.BlockSpec(memory_space=pltpu.HBM)
LIMIT = 60 * 1024 * 1024
TILE = 256
PIECES = 4
LAST = (((1,), (1,)), ((), ()))
F32 = jnp.float32
BF16 = jnp.bfloat16


def remote(src, dst, send, recv, axis, target):
    return pltpu.make_async_remote_copy(
        src_ref=src,
        dst_ref=dst,
        send_sem=send,
        recv_sem=recv,
        device_id={axis: target},
        device_id_type=MESH,
    )


def span(index, size):
    return pl.ds(pl.multiple_of(index * size, size), size)


def loop(low, high, body, **options):
    def step(i, carry):
        body(i)
        return carry

    lax.fori_loop(low, high, step, 0, **options)


def layer_kernel(n, bits, *refs):
    ids, comb, x_in, dy_in, g_in, u_in, d_in = refs[:7]
    in_grad, comb_grad, both_out, down_out = refs[7:11]
    x_all, dy_all, x_t, wg, wu, wd, slope, act_all = refs[11:19]
    h_all, h_t, pair_d, hid, rows_out, rows_got = refs[19:25]
    tables, comb_out, comb_got = refs[25:28]
    both_part, down_part = refs[28:30]
    both_got, down_got = refs[30 : 30 + bits], refs[30 + bits : 30 + 2 * bits]
    rest = refs[30 + 2 * bits :]
    load, a_send, a_recv, t_send, t_recv, r_send, r_recv, c_send, c_recv = rest[:9]
    b_send, b_recv, d_send, d_recv = rest[9:13]

    me = lax.axis_index("expert")
    rank = lax.axis_index("dp")
    replicas = 1 << bits
    half = replicas // 2
    rows = in_grad.shape[0]
    feature, width = wg.shape
    piece = feature // PIECES
    chunks = 2 * width // TILE
    both_rows, down_rows = both_out.shape[0], down_out.shape[0]
    bit = [lax.rem(rank // (1 << b), 2) for b in range(bits)]
    mate = [rank + (1 - 2 * bit[b]) * (1 << b) for b in range(bits)]
    orders = ([0] + list(range(1, bits)), [0] + list(range(bits - 1, 0, -1)))
    is_end = jnp.logical_or(me == 0, me == n - 1)
    is_mid = jnp.logical_not(is_end)

    loads = [
        pltpu.make_async_copy(src, dst, load.at[i])
        for i, (src, dst) in enumerate(
            (
                (x_in, x_all.at[span(me, rows)]),
                (dy_in, dy_all.at[span(me, rows)]),
                (g_in.at[0], wg),
                (u_in.at[0], wu),
                (d_in.at[0], wd),
            )
        )
    ]
    for item in loads:
        item.start()
    barrier = pltpu.get_barrier_semaphore()
    for k in range(1, n):
        pl.semaphore_signal(
            barrier, inc=1, device_id={"expert": lax.rem(me + k, n)}, device_id_type=MESH
        )
    for b in range(bits):
        pl.semaphore_signal(barrier, inc=1, device_id={"dp": mate[b]}, device_id_type=MESH)

    lane = lax.broadcasted_iota(jnp.int32, (rows, 128), 1)
    weight = jnp.where(lane == ids[:, 0:1], comb[:, 0:1], 0.0)
    for k in range(1, ids.shape[1]):
        weight = weight + jnp.where(lane == ids[:, k : k + 1], comb[:, k : k + 1], 0.0)
    tables[me] = weight.T[: tables.shape[1]]

    def view(p, block):
        if p is None:
            return x_all.at[span(block, rows)]
        return dy_all.at[span(block, rows), span(p, piece)]

    def index(p):
        return 0 if p is None else 1 + p

    def hop(p, side, s):
        step = 1 - 2 * side
        slot = view(p, jnp.clip(me - step * s, 0, n - 1))
        target = jnp.clip(me + step, 0, n - 1)
        i = index(p)
        return remote(slot, slot, a_send.at[i, side, s], a_recv.at[i, side, s], "expert", target)

    def arrival(p, side, s):
        step = 1 - 2 * side
        slot = view(p, jnp.clip(me - step * (s + 1), 0, n - 1))
        i = index(p)
        return remote(slot, slot, a_send.at[i, side, s], a_recv.at[i, side, s], "expert", me)

    def sends(side, s):
        if side == 0:
            return jnp.logical_and(me >= s, me + 1 < n)
        return jnp.logical_and(me + s < n, me >= 1)

    def passes(side):
        return jnp.where(side == 0, me + 1 < n, me >= 1)

    def table_copy(target):
        return remote(
            tables.at[me], tables.at[me], t_send.at[target], t_recv.at[me], "expert", target
        )

    def row_copy(target):
        return remote(
            rows_out.at[target],
            rows_got.at[me],
            r_send.at[target],
            r_recv.at[me],
            "expert",
            target,
        )

    def comb_copy(target):
        return remote(
            comb_out.at[target],
            comb_got.at[me],
            c_send.at[target],
            c_recv.at[me],
            "expert",
            target,
        )

    pl.semaphore_wait(barrier, n - 1 + bits)
    others = [lax.rem(me + k, n) for k in range(1, n)]
    for target in others:
        table_copy(target).start()
    loads[0].wait()
    for side in range(2):

        @pl.when(sends(side, 0))
        def _():
            hop(None, side, 0).start()

    loads[1].wait()
    for side in range(2):

        @pl.when(sends(side, 0))
        def _():
            for p in range(PIECES):
                hop(p, side, 0).start()

    for item in loads[2:]:
        item.wait()

    def coefficient(b):
        line = tables[b, pl.ds(me, 1), :]
        return jnp.broadcast_to(line, (128, rows)).T[:, 0:1]

    def forward(b):
        own = span(b, rows)
        coef = coefficient(b)

        def tile(j):
            cols = span(j, TILE)
            value = x_all[own, :]
            gate = jnp.dot(value, wg[:, cols], preferred_element_type=F32)
            up = jnp.dot(value, wu[:, cols], preferred_element_type=F32)
            sig = jax.nn.sigmoid(gate)
            act = gate * sig
            hidden = (act * up).astype(BF16)
            slope[own, cols] = up * (sig * (1.0 + gate * (1.0 - sig)))
            act_all[own, cols] = act
            h_all[own, cols] = hidden
            h_t[cols, own] = (coef * hidden.astype(F32)).T.astype(BF16)

        loop(0, width // TILE, tile)

        def turn(j):
            cols = span(j, TILE)
            x_t[cols, own] = x_all[own, cols].T

        loop(0, feature // TILE, turn)

    def gather_hidden(b, q):
        cols = span(q, piece)
        hid[...] += lax.dot_general(
            dy_all[span(b, rows), cols], wd[:, cols], LAST, preferred_element_type=F32
        )

    def slopes(b):
        own = span(b, rows)
        coef = coefficient(b)

        def tile(j, total):
            cols = span(j, TILE)
            grad = hid[:, cols]
            total = total + jnp.sum(h_all[own, cols].astype(F32) * grad, axis=1, keepdims=True)
            grad = coef * grad
            pair_d[own, cols] = (grad * slope[own, cols]).astype(BF16)
            pair_d[own, span(width // TILE + j, TILE)] = (grad * act_all[own, cols]).astype(BF16)
            return total

        total = lax.fori_loop(0, width // TILE, tile, jnp.zeros((rows, 1), F32))
        comb_out[b] = jnp.broadcast_to(total, (rows, 128)).T[:8]

    def input_rows(b):
        own = span(b, rows)

        def tile(j):
            cols = span(j, TILE)
            value = lax.dot_general(
                pair_d[own, :width], wg[cols, :], LAST, preferred_element_type=F32
            )
            value = value + lax.dot_general(
                pair_d[own, width:], wu[cols, :], LAST, preferred_element_type=F32
            )
            rows_out[b, :, cols] = value.astype(BF16)

        loop(0, feature // TILE, tile)

    def send_rows(b):
        row_copy(b).start()
        comb_copy(b).start()

    def distance(d):
        low = jnp.where(jnp.logical_or(d == 0, me >= d), 0, 1)
        high = jnp.where(jnp.logical_and(d > 0, me + d < n), 2, 1)

        def source(side):
            return jnp.clip(me + d * (2 * side - 1), 0, n - 1)

        def take(side):
            @pl.when(d > 0)
            def _():
                arrival(None, side, d - 1).wait_recv()
                b = source(side)
                remote(
                    tables.at[b], tables.at[b], t_send.at[b], t_recv.at[b], "expert", me
                ).wait_recv()

                @pl.when(passes(side))
                def _():
                    hop(None, side, d).start()

        loop(low, high, take)
        loop(low, high, lambda side: forward(source(side)))

        def back(side):
            b = source(side)
            hid[...] = jnp.zeros_like(hid)

            def part(q):
                @pl.when(d > 0)
                def _():
                    arrival(q, side, d - 1).wait_recv()

                    @pl.when(passes(side))
                    def _():
                        hop(q, side, d).start()

                gather_hidden(b, q)

            loop(0, PIECES, part)
            slopes(b)
            input_rows(b)

            @pl.when(jnp.logical_and(is_end, d > 0))
            def _():
                send_rows(b)

        @pl.when(d < n - 1)
        def _():
            loop(low, high, back)

    loop(0, n, distance)

    for target in others:
        inner = jnp.logical_and(target > 0, target < n - 1)

        @pl.when(jnp.logical_and(is_mid, inner))
        def _():
            send_rows(target)

    def rank_of(way, place):
        value = 0
        for i, b in enumerate(orders[way]):
            value = value + lax.rem(place // (1 << (bits - 1 - i)), 2) * (1 << b)
        return value

    def place_of(way, who):
        value = 0
        for i, b in enumerate(orders[way]):
            value = value + lax.rem(who // (1 << b), 2) * (1 << (bits - 1 - i))
        return value

    kinds = {
        "both": (both_part, both_got, b_send, b_recv),
        "down": (down_part, down_got, d_send, d_recv),
    }

    def base(way, i):
        value = 0
        for j in range(i):
            value = value + bit[orders[way][j]] * (replicas >> (j + 1))
        return value

    def stage(kind, c, way, i):
        part, got, send, recv = kinds[kind]
        b = orders[way][i]
        count = replicas >> (i + 1)
        start = base(way, i) + (1 - bit[b]) * count
        return remote(
            part.at[c, pl.ds(start, count)],
            got[i].at[c],
            send.at[c, i],
            recv.at[c, i],
            "dp",
            mate[b],
        )

    def combine(kind, c, way, i):
        part, got, _, _ = kinds[kind]
        count = replicas >> (i + 1)
        start = base(way, i + 1)
        stage(kind, c, way, i).wait_recv()
        if i == bits - 1:
            total = part[c, start].astype(F32) + got[i][c, 0].astype(F32)
            if kind == "both":
                both_out[:, span(c, TILE)] = total.astype(BF16)
            else:
                down_out[:, span(c, piece)] = total.astype(BF16)
            return

        def add(k):
            total = part[c, start + k].astype(F32) + got[i][c, k].astype(F32)
            part[c, start + k] = total.astype(BF16)

        loop(0, count, add)
        stage(kind, c, way, i + 1).start()

    def both_chunk(c, way):
        def place(j):
            where = lax.rem(j + (1 - bit[0]) * half, replicas)
            lines = span(rank_of(way, where), both_rows)
            value = jnp.dot(x_t[lines, :], pair_d[:, span(c, TILE)], preferred_element_type=F32)
            both_part[c, where] = value.astype(BF16)

        loop(0, half, place, unroll=2)
        stage("both", c, way, 0).start()
        loop(half, replicas, place, unroll=2)

    def down_chunk(q, way):
        cols = span(q, piece)
        if down_rows % 16 == 0:

            def place(j):
                where = lax.rem(j + (1 - bit[0]) * half, replicas)
                lines = span(rank_of(way, where), down_rows)
                value = jnp.dot(h_t[lines, :], dy_all[:, cols], preferred_element_type=F32)
                down_part[q, where] = value.astype(BF16)

            loop(0, half, place, unroll=2)
            stage("down", q, way, 0).start()
            loop(half, replicas, place, unroll=2)
        else:

            def place(j):
                lines = span(j, 2 * down_rows)
                value = jnp.dot(h_t[lines, :], dy_all[:, cols], preferred_element_type=F32)
                for k in range(2):
                    some = value[k * down_rows : (k + 1) * down_rows]
                    down_part[q, place_of(way, 2 * j + k)] = some.astype(BF16)

            loop(0, half, place)
            stage("down", q, way, 0).start()

    last = jnp.clip(n - 1 - me, 0, n - 1)
    last_side = jnp.where(me == n - 1, 0, 1)

    @pl.when(is_end)
    def _():
        hid[...] = jnp.zeros_like(hid)

    def early(k):
        for way in range(2):
            q = 2 * k + way

            @pl.when(is_end)
            def _():
                arrival(q, last_side, n - 2).wait_recv()
                gather_hidden(last, q)

            down_chunk(q, way)
            if way == 1:
                combine("down", q - 1, 0, 0)
            else:

                @pl.when(k > 0)
                def _():
                    combine("down", q - 1, 1, 0)

    loop(0, PIECES // 2, early)

    @pl.when(is_end)
    def _():
        slopes(last)

    combine("down", PIECES - 1, 1, 0)

    def late(k):
        for way in range(2):
            c = 2 * k + way
            both_chunk(c, way)
            if way == 1:
                combine("both", c - 1, 0, 0)
            else:

                @pl.when(k > 0)
                def _():
                    combine("both", c - 1, 1, 0)

            @pl.when(jnp.logical_and(k > 0, k <= PIECES // 2))
            def _():
                combine("down", c - 2, way, 1)

    loop(0, chunks // 2, late)
    combine("both", chunks - 1, 1, 0)
    for q in range(max(0, chunks - 2), PIECES):
        combine("down", q, q % 2, 1)

    for side in range(2):
        for s in range(n - 1):

            @pl.when(sends(side, s))
            def _():
                hop(None, side, s).wait_send()
                for p in range(PIECES):
                    hop(p, side, s).wait_send()

    for target in others:
        outer = jnp.logical_or(target == 0, target == n - 1)

        @pl.when(jnp.logical_and(is_mid, outer))
        def _():
            send_rows(target)

    @pl.when(is_end)
    def _():
        input_rows(last)
        send_rows(last)

    for i in range(1, bits):
        for way in range(2):
            if i > 1:
                loop(0, PIECES // 2, lambda k: combine("down", 2 * k + way, way, i))
        if i < bits:

            def step(k):
                for way in range(2):
                    combine("both", 2 * k + way, way, i)

            loop(0, chunks // 2, step)

    for b in others:
        remote(
            rows_got.at[b], rows_got.at[b], r_send.at[b], r_recv.at[b], "expert", me
        ).wait_recv()
        remote(
            comb_got.at[b], comb_got.at[b], c_send.at[b], c_recv.at[b], "expert", me
        ).wait_recv()

    def total_rows(j):
        cols = span(j, TILE)
        total = rows_out[me, :, cols].astype(F32)
        for b in others:
            total = total + rows_got[b, :, cols].astype(F32)
        in_grad[:, cols] = total.astype(BF16)

    loop(0, feature // TILE, total_rows)

    def spread(line):
        return jnp.broadcast_to(line, (128, rows)).T[:, 0:1]

    picked = jnp.where(ids[...] == me, spread(comb_out[me, 0:1, :]), 0.0)
    for b in others:
        picked = picked + jnp.where(ids[...] == b, spread(comb_got[b, 0:1, :]), 0.0)
    comb_grad[...] = picked

    for target in others:
        table_copy(target).wait_send()
        row_copy(target).wait_send()
        comb_copy(target).wait_send()
    for kind, count in (("both", chunks), ("down", PIECES)):

        def drain(k):
            for way in range(2):
                for i in range(bits):
                    stage(kind, 2 * k + way, way, i).wait_send()

        loop(0, count // 2, drain)


def shards(tokens, cotangent, expert_ids, combine, w_gate, w_up, w_down):
    n = lax.axis_size("expert")
    replicas = lax.axis_size("dp")
    bits = replicas.bit_length() - 1
    rows, top = expert_ids.shape
    feature = tokens.shape[1]
    width = w_gate.shape[2]
    everyone = n * rows
    chunks = 2 * width // TILE
    piece = feature // PIECES
    both_rows, down_rows = feature // replicas, width // replicas
    table = -(-n // 8) * 8
    outs = [
        jax.ShapeDtypeStruct((rows, feature), BF16),
        jax.ShapeDtypeStruct((rows, top), F32),
        jax.ShapeDtypeStruct((both_rows, 2 * width), BF16),
        jax.ShapeDtypeStruct((down_rows, feature), BF16),
    ]
    scratch = [
        pltpu.VMEM((everyone, feature), BF16),
        pltpu.VMEM((everyone, feature), BF16),
        pltpu.VMEM((feature, everyone), BF16),
        pltpu.VMEM((feature, width), BF16),
        pltpu.VMEM((feature, width), BF16),
        pltpu.VMEM((width, feature), BF16),
        pltpu.VMEM((everyone, width), F32),
        pltpu.VMEM((everyone, width), F32),
        pltpu.VMEM((everyone, width), BF16),
        pltpu.VMEM((width, everyone), BF16),
        pltpu.VMEM((everyone, 2 * width), BF16),
        pltpu.VMEM((rows, width), F32),
        pltpu.VMEM((n, rows, feature), BF16),
        pltpu.VMEM((n, rows, feature), BF16),
        pltpu.VMEM((n, table, rows), F32),
        pltpu.VMEM((n, 8, rows), F32),
        pltpu.VMEM((n, 8, rows), F32),
        pltpu.VMEM((chunks, replicas, both_rows, TILE), BF16),
        pltpu.VMEM((PIECES, replicas, down_rows, piece), BF16),
    ]
    for i in range(bits):
        scratch.append(pltpu.VMEM((chunks, replicas >> (i + 1), both_rows, TILE), BF16))
    for i in range(bits):
        scratch.append(pltpu.VMEM((PIECES, replicas >> (i + 1), down_rows, piece), BF16))
    scratch += [pltpu.SemaphoreType.DMA((5,))]
    scratch += [pltpu.SemaphoreType.DMA((1 + PIECES, 2, n))] * 2
    scratch += [pltpu.SemaphoreType.DMA((n,))] * 6
    scratch += [pltpu.SemaphoreType.DMA((chunks, bits))] * 2
    scratch += [pltpu.SemaphoreType.DMA((PIECES, bits))] * 2
    input_grad, combine_grad, both, down = pl.pallas_call(
        functools.partial(layer_kernel, n, bits),
        out_shape=outs,
        in_specs=[VMEM] * 2 + [HBM] * 5,
        out_specs=[VMEM] * 4,
        scratch_shapes=scratch,
        compiler_params=pltpu.CompilerParams(
            collective_id=0, has_side_effects=True, vmem_limit_bytes=LIMIT
        ),
        name="layer",
    )(expert_ids, combine, tokens, cotangent, w_gate, w_up, w_down)
    return (input_grad, combine_grad, both[None, :, :width], both[None, :, width:], down[None])


def solution(mesh):
    by_token = P(("dp", "expert"), None)
    by_expert = P("expert", None, None)
    by_row = P("expert", "dp", None)
    return jax.shard_map(
        shards,
        mesh=mesh,
        in_specs=(by_token,) * 4 + (by_expert,) * 3,
        out_specs=(by_token, by_token, by_row, by_row, by_row),
        check_vma=False,
    )
```

time: 171 us -> 128 us (0.75)
  matrix products: 25.7 us -> 0 us
  Pallas kernels: 130 us -> 117 us
  other arithmetic: 4.01 us -> 0 us
    dot_general x8 -> x0, matrix products: 25.7 us -> none  [the longest x1 5.63 us: shards(): both = lax.dot_general(x, paired, first, preferred_element_type=jnp.float32)]
    pallas_call x2 -> x1, Pallas kernels: 130 us -> 117 us  [shards(): pl.pallas_call(functools.partial(layer_kernel, n, bits), out_shape=outs,...]
    convert_element_type x2 -> x0, other arithmetic: 2.55 us -> none  [shards(): scaled = (coeff * dy.astype(jnp.float32)).astype(jnp.bfloat16)]
    unnamed x22 -> x5, local copies, waits for them, and re-layouts: 5.69 us -> 7.95 us
    gather x2 -> x0, local copies, waits for them, and re-layouts: 1.9 us -> none  [the longest x1 1.34 us: shards(): comb = combs[sources, 0]]
where the time goes in v1:
time: 128 us
  Pallas kernels  117 us (91%)
  local copies, waits for them, and re-layouts  9.99 us (8%)
    pallas_call x1, Pallas kernels, shards(): pl.pallas_call(functools.partial(layer_kernel, n, bits), out_shape=outs,...  117 us
    unnamed x5, local copies, waits for them, and re-layouts  7.95 us

profile of v1, /device:TPU:0, one launch (start us, length us, event | category | flops | bytes accessed | tf_op | source)
XLA Modules:
  0.0 127.6 jit_solution(18385153812396677661)
XLA Ops:
  0.6 1.4 %copy.12.refs_0_ = s32[128,2]{1,0:T(8,128)} copy(s32[128,2]{0,1:T(2,128)} %param.9) | data formatting | bytes 2048 | tf_op args[2]
  2.0 1.4 %copy.13.refs_1_ = f32[128,2]{1,0:T(8,128)} copy(f32[128,2]{0,1:T(2,128)} %param.10) | data formatting | bytes 2048 | tf_op args[3]
  3.5 117.0 %layer.1 = (bf16[128,2048]{1,0:T(8,128)(2,1)}, f32[128,2]{1,0:T(8,128)}, bf16[256,1536]{1,0:T(8,128)(2,1)}, bf16[96,2048]{1,0:T(8,128)(2,1)}) custom-call(s32[128,2]{1,0:T(8,128)} %copy.12.refs_0_, f32[128,2]{1,0:T(8,128)} %copy.13.refs_1_, bf16[128,2048]{1,0:T(8,128)(2,1)} %refs_2_.1, bf16[128,2048]{1,0:T(8,128)(2,1)} %refs_3_.1, ...), custom_call_target="tpu_custom_call" | custom-call | tf_op jit(solution)/shard_map/layer/pallas_call | solution.py:570
  120.5 1.5 %copy.14 = f32[128,2]{0,1:T(2,128)} copy(f32[128,2]{1,0:T(8,128)} %get-tuple-element.14) | data formatting | bytes 2048
  121.9 2.0 %slice_bitcast_fusion = (bf16[1,256,768]{2,1,0:T(8,128)(2,1)}, bf16[1,256,768]{2,1,0:T(8,128)(2,1)}) fusion(bf16[256,1536]{1,0:T(8,128)(2,1)} %get-tuple-element.11), kind=kLoop, calls=%fused_computation | loop fusion | bytes 1572864 | tf_op jit(solution)/shard_map/broadcast_in_dim | solution.py:581
  124.0 1.9 %copy.17 = bf16[128,2048]{1,0:T(8,128)(2,1)} copy(bf16[128,2048]{1,0:T(8,128)(2,1)} %get-tuple-element.25) | data formatting | bytes 1048576
  125.8 1.8 %copy.18 = bf16[1,96,2048]{2,1,0:T(8,128)(2,1)} copy(bf16[1,96,2048]{2,1,0:T(8,128)(2,1)} %bitcast.5) | data formatting | bytes 786432

commit v2 on v1

--- a/solution.py
+++ b/solution.py
@@ -9,8 +9,9 @@
 MESH = pl.DeviceIdType.MESH
 VMEM = pl.BlockSpec(memory_space=pltpu.VMEM)
 HBM = pl.BlockSpec(memory_space=pltpu.HBM)
-LIMIT = 60 * 1024 * 1024
+LIMIT = 50 * 1024 * 1024
 TILE = 256
+WIDE = 512
 PIECES = 4
 LAST = (((1,), (1,)), ((), ()))
 F32 = jnp.float32
@@ -50,7 +51,7 @@
     both_got, down_got = refs[30 : 30 + bits], refs[30 + bits : 30 + 2 * bits]
     rest = refs[30 + 2 * bits :]
     load, a_send, a_recv, t_send, t_recv, r_send, r_recv, c_send, c_recv = rest[:9]
-    b_send, b_recv, d_send, d_recv = rest[9:13]
+    b_send, b_recv, d_send, d_recv, f_send, f_recv = rest[9:15]
 
     me = lax.axis_index("expert")
     rank = lax.axis_index("dp")
@@ -71,8 +72,6 @@
         pltpu.make_async_copy(src, dst, load.at[i])
         for i, (src, dst) in enumerate(
             (
-                (x_in, x_all.at[span(me, rows)]),
-                (dy_in, dy_all.at[span(me, rows)]),
                 (g_in.at[0], wg),
                 (u_in.at[0], wu),
                 (d_in.at[0], wd),
@@ -89,11 +88,11 @@
     for b in range(bits):
         pl.semaphore_signal(barrier, inc=1, device_id={"dp": mate[b]}, device_id_type=MESH)
 
-    lane = lax.broadcasted_iota(jnp.int32, (rows, 128), 1)
-    weight = jnp.where(lane == ids[:, 0:1], comb[:, 0:1], 0.0)
-    for k in range(1, ids.shape[1]):
-        weight = weight + jnp.where(lane == ids[:, k : k + 1], comb[:, k : k + 1], 0.0)
-    tables[me] = weight.T[: tables.shape[1]]
+    expert = lax.broadcasted_iota(jnp.int32, tables.shape[1:], 0)
+    weight = jnp.where(expert == ids[0:1, :], comb[0:1, :], 0.0)
+    for k in range(1, ids.shape[0]):
+        weight = weight + jnp.where(expert == ids[k : k + 1, :], comb[k : k + 1, :], 0.0)
+    tables[me] = weight
 
     def view(p, block):
         if p is None:
@@ -103,12 +102,15 @@
     def index(p):
         return 0 if p is None else 1 + p
 
-    def hop(p, side, s):
+    def hop(p, side, s, own=False):
         step = 1 - 2 * side
         slot = view(p, jnp.clip(me - step * s, 0, n - 1))
         target = jnp.clip(me + step, 0, n - 1)
         i = index(p)
-        return remote(slot, slot, a_send.at[i, side, s], a_recv.at[i, side, s], "expert", target)
+        src = slot
+        if own:
+            src = x_in if p is None else dy_in.at[:, span(p, piece)]
+        return remote(src, slot, a_send.at[i, side, s], a_recv.at[i, side, s], "expert", target)
 
     def arrival(p, side, s):
         step = 1 - 2 * side
@@ -139,6 +141,20 @@
             target,
         )
 
+    fold = n == 4
+    ally = n - 1 - me
+    near = jnp.where(2 * me < n, 0, n - 1)
+    far = n - 1 - near
+
+    def fold_copy():
+        return remote(
+            rows_out.at[far], rows_got.at[ally], f_send.at[0], f_recv.at[0], "expert", ally
+        )
+
+    def folded():
+        slot = rows_got.at[me]
+        return remote(slot, slot, f_send.at[0], f_recv.at[0], "expert", me)
+
     def comb_copy(target):
         return remote(
             comb_out.at[target],
@@ -153,22 +169,16 @@
     others = [lax.rem(me + k, n) for k in range(1, n)]
     for target in others:
         table_copy(target).start()
-    loads[0].wait()
-    for side in range(2):
-
-        @pl.when(sends(side, 0))
-        def _():
-            hop(None, side, 0).start()
-
-    loads[1].wait()
-    for side in range(2):
-
-        @pl.when(sends(side, 0))
-        def _():
-            for p in range(PIECES):
-                hop(p, side, 0).start()
-
-    for item in loads[2:]:
+    for p in [None] + list(range(PIECES)):
+        for side in range(2):
+
+            @pl.when(sends(side, 0))
+            def _():
+                hop(p, side, 0, True).start()
+
+    x_all[span(me, rows), :] = x_in[...]
+    dy_all[span(me, rows), :] = dy_in[...]
+    for item in loads:
         item.wait()
 
     def coefficient(b):
@@ -222,20 +232,14 @@
         total = lax.fori_loop(0, width // TILE, tile, jnp.zeros((rows, 1), F32))
         comb_out[b] = jnp.broadcast_to(total, (rows, 128)).T[:8]
 
-    def input_rows(b):
+    def input_tile(b, j):
         own = span(b, rows)
-
-        def tile(j):
-            cols = span(j, TILE)
-            value = lax.dot_general(
-                pair_d[own, :width], wg[cols, :], LAST, preferred_element_type=F32
-            )
-            value = value + lax.dot_general(
-                pair_d[own, width:], wu[cols, :], LAST, preferred_element_type=F32
-            )
-            rows_out[b, :, cols] = value.astype(BF16)
-
-        loop(0, feature // TILE, tile)
+        cols = span(j, WIDE)
+        value = lax.dot_general(pair_d[own, :width], wg[cols, :], LAST, preferred_element_type=F32)
+        value = value + lax.dot_general(
+            pair_d[own, width:], wu[cols, :], LAST, preferred_element_type=F32
+        )
+        rows_out[b, :, cols] = value.astype(BF16)
 
     def send_rows(b):
         row_copy(b).start()
@@ -281,7 +285,7 @@
 
             loop(0, PIECES, part)
             slopes(b)
-            input_rows(b)
+            loop(0, feature // WIDE, functools.partial(input_tile, b))
 
             @pl.when(jnp.logical_and(is_end, d > 0))
             def _():
@@ -293,12 +297,20 @@
 
     loop(0, n, distance)
 
-    for target in others:
-        inner = jnp.logical_and(target > 0, target < n - 1)
-
-        @pl.when(jnp.logical_and(is_mid, inner))
+    if fold:
+
+        @pl.when(is_mid)
         def _():
-            send_rows(target)
+            fold_copy().start()
+            send_rows(ally)
+
+    else:
+        for target in others:
+            inner = jnp.logical_and(target > 0, target < n - 1)
+
+            @pl.when(jnp.logical_and(is_mid, inner))
+            def _():
+                send_rows(target)
 
     def rank_of(way, place):
         value = 0
@@ -403,28 +415,30 @@
     def early(k):
         for way in range(2):
             q = 2 * k + way
+            if way == 1:
+                combine("down", q - 1, 0, 0)
+            else:
+
+                @pl.when(k > 0)
+                def _():
+                    combine("down", q - 1, 1, 0)
 
             @pl.when(is_end)
             def _():
                 arrival(q, last_side, n - 2).wait_recv()
                 gather_hidden(last, q)
 
+            if way == 1:
+
+                @pl.when(jnp.logical_and(is_end, q == PIECES - 1))
+                def _():
+                    slopes(last)
+
             down_chunk(q, way)
-            if way == 1:
-                combine("down", q - 1, 0, 0)
-            else:
-
-                @pl.when(k > 0)
-                def _():
-                    combine("down", q - 1, 1, 0)
 
     loop(0, PIECES // 2, early)
-
-    @pl.when(is_end)
-    def _():
-        slopes(last)
-
-    combine("down", PIECES - 1, 1, 0)
+    wide = feature // WIDE
+    share = -(-wide // (chunks - 2))
 
     def late(k):
         for way in range(2):
@@ -434,9 +448,20 @@
                 combine("both", c - 1, 0, 0)
             else:
 
+                @pl.when(k == 0)
+                def _():
+                    combine("down", PIECES - 1, 1, 0)
+
                 @pl.when(k > 0)
                 def _():
                     combine("both", c - 1, 1, 0)
+
+            for t in range(share):
+                j = share * (c - 2) + t
+
+                @pl.when(jnp.logical_and(is_end, jnp.logical_and(k > 0, j < wide)))
+                def _():
+                    input_tile(last, j)
 
             @pl.when(jnp.logical_and(k > 0, k <= PIECES // 2))
             def _():
@@ -446,6 +471,10 @@
     combine("both", chunks - 1, 1, 0)
     for q in range(max(0, chunks - 2), PIECES):
         combine("down", q, q % 2, 1)
+
+    @pl.when(is_end)
+    def _():
+        send_rows(last)
 
     for side in range(2):
         for s in range(n - 1):
@@ -456,59 +485,114 @@
                 for p in range(PIECES):
                     hop(p, side, s).wait_send()
 
-    for target in others:
-        outer = jnp.logical_or(target == 0, target == n - 1)
-
-        @pl.when(jnp.logical_and(is_mid, outer))
+    if fold:
+
+        @pl.when(is_mid)
         def _():
-            send_rows(target)
-
-    @pl.when(is_end)
-    def _():
-        input_rows(last)
-        send_rows(last)
-
-    for i in range(1, bits):
-        for way in range(2):
-            if i > 1:
+            folded().wait_recv()
+
+            def add(j):
+                cols = span(j, TILE)
+                total = rows_out[near, :, cols].astype(F32) + rows_got[me, :, cols].astype(F32)
+                rows_out[near, :, cols] = total.astype(BF16)
+
+            loop(0, feature // TILE, add)
+            row_copy(near).start()
+            comb_copy(near).start()
+            comb_copy(far).start()
+
+    else:
+        for target in others:
+            outer = jnp.logical_or(target == 0, target == n - 1)
+
+            @pl.when(jnp.logical_and(is_mid, outer))
+            def _():
+                send_rows(target)
+
+    for i in range(1, bits - 1):
+        if i > 1:
+            for way in range(2):
                 loop(0, PIECES // 2, lambda k: combine("down", 2 * k + way, way, i))
-        if i < bits:
-
-            def step(k):
-                for way in range(2):
-                    combine("both", 2 * k + way, way, i)
-
-            loop(0, chunks // 2, step)
+
+        def step(k):
+            for way in range(2):
+                combine("both", 2 * k + way, way, i)
+
+        loop(0, chunks // 2, step)
+
+    for way in range(2):
+        loop(0, PIECES // 2, lambda k: combine("down", 2 * k + way, way, bits - 1))
+
+    def takes_row(b):
+        if not fold:
+            return b >= 0
+        return jnp.logical_or(is_mid, b != jnp.where(me == 0, n - 2, 1))
+
+    def gives_row(target):
+        if not fold:
+            return target >= 0
+        return jnp.logical_or(is_end, target != far)
 
     for b in others:
-        remote(
-            rows_got.at[b], rows_got.at[b], r_send.at[b], r_recv.at[b], "expert", me
-        ).wait_recv()
+
+        @pl.when(takes_row(b))
+        def _():
+            remote(
+                rows_got.at[b], rows_got.at[b], r_send.at[b], r_recv.at[b], "expert", me
+            ).wait_recv()
+
         remote(
             comb_got.at[b], comb_got.at[b], c_send.at[b], c_recv.at[b], "expert", me
         ).wait_recv()
 
-    def total_rows(j):
-        cols = span(j, TILE)
-        total = rows_out[me, :, cols].astype(F32)
-        for b in others:
-            total = total + rows_got[b, :, cols].astype(F32)
-        in_grad[:, cols] = total.astype(BF16)
-
-    loop(0, feature // TILE, total_rows)
-
-    def spread(line):
-        return jnp.broadcast_to(line, (128, rows)).T[:, 0:1]
-
-    picked = jnp.where(ids[...] == me, spread(comb_out[me, 0:1, :]), 0.0)
+    def total_rows(who):
+        def tile(j):
+            cols = span(j, TILE)
+            total = rows_out[me, :, cols].astype(F32)
+            for b in who:
+                total = total + rows_got[b, :, cols].astype(F32)
+            in_grad[:, cols] = total.astype(BF16)
+
+        loop(0, feature // TILE, tile)
+
+    if fold:
+
+        @pl.when(is_end)
+        def _():
+            total_rows([n - 1 - me, jnp.where(me == 0, 1, n - 2)])
+
+        @pl.when(is_mid)
+        def _():
+            total_rows(others)
+
+    else:
+        total_rows(others)
+
+    picked = jnp.where(ids[...] == me, comb_out[me, 0:1, :], 0.0)
     for b in others:
-        picked = picked + jnp.where(ids[...] == b, spread(comb_got[b, 0:1, :]), 0.0)
+        picked = picked + jnp.where(ids[...] == b, comb_got[b, 0:1, :], 0.0)
     comb_grad[...] = picked
+
+    def finish(k):
+        for way in range(2):
+            combine("both", 2 * k + way, way, bits - 1)
+
+    loop(0, chunks // 2, finish)
 
     for target in others:
         table_copy(target).wait_send()
-        row_copy(target).wait_send()
         comb_copy(target).wait_send()
+
+        @pl.when(gives_row(target))
+        def _():
+            row_copy(target).wait_send()
+
+    if fold:
+
+        @pl.when(is_mid)
+        def _():
+            fold_copy().wait_send()
+
     for kind, count in (("both", chunks), ("down", PIECES)):
 
         def drain(k):
@@ -517,6 +601,44 @@
                     stage(kind, 2 * k + way, way, i).wait_send()
 
         loop(0, count // 2, drain)
+
+
+def deliver_kernel(rows, comb, both, down, *refs):
+    outs, sems = refs[:-1], refs[-1]
+    width = outs[2].shape[2]
+    copies = []
+    for src, dst in (
+        (rows, outs[0]),
+        (both.at[:, pl.ds(0, width)], outs[2].at[0]),
+        (both.at[:, pl.ds(width, width)], outs[3].at[0]),
+        (down, outs[4].at[0]),
+        (comb, outs[1]),
+    ):
+        copies.append(pltpu.make_async_copy(src, dst, sems.at[len(copies)]))
+        copies[-1].start()
+    for copy in copies:
+        copy.wait()
+
+
+def deliver(rows, comb, both, down):
+    width = both.shape[1] // 2
+    outs = [
+        jax.ShapeDtypeStruct(rows.shape, BF16),
+        jax.ShapeDtypeStruct(comb.shape, F32),
+        jax.ShapeDtypeStruct((1, both.shape[0], width), BF16),
+        jax.ShapeDtypeStruct((1, both.shape[0], width), BF16),
+        jax.ShapeDtypeStruct((1,) + down.shape, BF16),
+    ]
+    input_grad, combine_grad, gate_grad, up_grad, down_grad = pl.pallas_call(
+        deliver_kernel,
+        out_shape=outs,
+        in_specs=[VMEM] * 4,
+        out_specs=[HBM] * 5,
+        scratch_shapes=[pltpu.SemaphoreType.DMA((5,))],
+        compiler_params=pltpu.CompilerParams(vmem_limit_bytes=8 * 1024 * 1024),
+        name="deliver",
+    )(rows, comb, both, down)
+    return (input_grad, combine_grad.T, gate_grad, up_grad, down_grad)
 
 
 def shards(tokens, cotangent, expert_ids, combine, w_gate, w_up, w_down):
@@ -533,7 +655,7 @@
     table = -(-n // 8) * 8
     outs = [
         jax.ShapeDtypeStruct((rows, feature), BF16),
-        jax.ShapeDtypeStruct((rows, top), F32),
+        jax.ShapeDtypeStruct((top, rows), F32),
         jax.ShapeDtypeStruct((both_rows, 2 * width), BF16),
         jax.ShapeDtypeStruct((down_rows, feature), BF16),
     ]
@@ -562,23 +684,24 @@
         scratch.append(pltpu.VMEM((chunks, replicas >> (i + 1), both_rows, TILE), BF16))
     for i in range(bits):
         scratch.append(pltpu.VMEM((PIECES, replicas >> (i + 1), down_rows, piece), BF16))
-    scratch += [pltpu.SemaphoreType.DMA((5,))]
+    scratch += [pltpu.SemaphoreType.DMA((3,))]
     scratch += [pltpu.SemaphoreType.DMA((1 + PIECES, 2, n))] * 2
     scratch += [pltpu.SemaphoreType.DMA((n,))] * 6
     scratch += [pltpu.SemaphoreType.DMA((chunks, bits))] * 2
     scratch += [pltpu.SemaphoreType.DMA((PIECES, bits))] * 2
+    scratch += [pltpu.SemaphoreType.DMA((1,))] * 2
     input_grad, combine_grad, both, down = pl.pallas_call(
         functools.partial(layer_kernel, n, bits),
         out_shape=outs,
-        in_specs=[VMEM] * 2 + [HBM] * 5,
+        in_specs=[VMEM] * 4 + [HBM] * 3,
         out_specs=[VMEM] * 4,
         scratch_shapes=scratch,
         compiler_params=pltpu.CompilerParams(
             collective_id=0, has_side_effects=True, vmem_limit_bytes=LIMIT
         ),
         name="layer",
-    )(expert_ids, combine, tokens, cotangent, w_gate, w_up, w_down)
-    return (input_grad, combine_grad, both[None, :, :width], both[None, :, width:], down[None])
+    )(expert_ids.T, combine.T, tokens, cotangent, w_gate, w_up, w_down)
+    return deliver(input_grad, combine_grad, both, down)
 
 
 def solution(mesh):

time: 128 us -> 122 us (0.953)
  local copies, waits for them, and re-layouts: 9.99 us -> 3.43 us
    unnamed x5 -> x8, local copies, waits for them, and re-layouts: 7.95 us -> 3.43 us
    broadcast_in_dim x1 -> x0, local copies, waits for them, and re-layouts: 2.04 us -> none  [shards(): both[None, :, width:]]
where the time goes in v2:
time: 122 us; the launch traced here: 121 us
  Pallas kernels  117 us (96%)
  local copies, waits for them, and re-layouts  3.43 us (3%)
    pallas_call x1, Pallas kernels, shards(): pl.pallas_call(functools.partial(layer_kernel, n, bits), out_shape=outs,...  116 us
    unnamed x8, local copies, waits for them, and re-layouts  3.43 us

profile of v2, /device:TPU:0, one launch (start us, length us, event | category | flops | bytes accessed | tf_op | source)
XLA Modules:
  0.0 121.4 jit_solution(14281583855061190518)
XLA Ops:
  0.6 0.0 copy-start
  0.6 1.0 copy-done
  1.7 0.0 copy-start.1
  1.7 1.0 copy-done.1
  2.7 0.0 copy-start.2
  2.7 0.7 copy-done.2
  3.4 0.0 copy-start.3
  3.4 0.7 copy-done.3
  4.1 116.1 %layer.1 = (bf16[128,2048]{1,0:T(8,128)(2,1)S(1)}, f32[2,128]{1,0:T(2,128)S(1)}, bf16[256,1536]{1,0:T(8,128)(2,1)S(1)}, bf16[96,2048]{1,0:T(8,128)(2,1)S(1)}) custom-call(s32[2,128]{1,0:T(2,128)S(1)} %bitcast.3, f32[2,128]{1,0:T(2,128)S(1)} %bitcast.4, bf16[128,2048]{1,0:T(8,128)(2,1)S(1)} %copy-done, bf16[128,2048]{1,0:T(8,128)(2,1)S(1)} %copy-done.1, ...), custom_call_target="tpu_custom_call" | custom-call | tf_op jit(solution)/shard_map/layer/pallas_call | solution.py:693
  120.2 1.2 %deliver.1 = (bf16[128,2048]{1,0:T(8,128)(2,1)}, f32[2,128]{1,0:T(2,128)}, bf16[1,256,768]{2,1,0:T(8,128)(2,1)}, bf16[1,256,768]{2,1,0:T(8,128)(2,1)}, bf16[1,96,2048]{2,1,0:T(8,128)(2,1)}) custom-call(bf16[128,2048]{1,0:T(8,128)(2,1)S(1)} %get-tuple-element.14.rows, f32[2,128]{1,0:T(2,128)S(1)} %get-tuple-element.15.comb, ...), custom_call_target="tpu_custom_call" | custom-call | tf_op jit(solution)/shard_map/deliver/pallas_call | solution.py:632
Async XLA Ops:
  0.6 1.0 copy-start
  1.7 1.0 copy-start.1
  2.7 0.7 copy-start.2
  3.4 0.7 copy-start.3

commit v3 on v2

--- a/solution.py
+++ b/solution.py
@@ -312,12 +312,6 @@
             def _():
                 send_rows(target)
 
-    def rank_of(way, place):
-        value = 0
-        for i, b in enumerate(orders[way]):
-            value = value + lax.rem(place // (1 << (bits - 1 - i)), 2) * (1 << b)
-        return value
-
     def place_of(way, who):
         value = 0
         for i, b in enumerate(orders[way]):
@@ -340,70 +334,76 @@
         b = orders[way][i]
         count = replicas >> (i + 1)
         start = base(way, i) + (1 - bit[b]) * count
+        pick = slice(None) if i == 0 else way
         return remote(
-            part.at[c, pl.ds(start, count)],
-            got[i].at[c],
-            send.at[c, i],
-            recv.at[c, i],
+            part.at[c, pick, pl.ds(start, count)],
+            got[i].at[c, pick],
+            send.at[c, i, way],
+            recv.at[c, i, way],
             "dp",
             mate[b],
         )
 
-    def combine(kind, c, way, i):
+    def combine(kind, c, i):
         part, got, _, _ = kinds[kind]
         count = replicas >> (i + 1)
-        start = base(way, i + 1)
-        stage(kind, c, way, i).wait_recv()
-        if i == bits - 1:
-            total = part[c, start].astype(F32) + got[i][c, 0].astype(F32)
-            if kind == "both":
-                both_out[:, span(c, TILE)] = total.astype(BF16)
-            else:
-                down_out[:, span(c, piece)] = total.astype(BF16)
-            return
-
-        def add(k):
-            total = part[c, start + k].astype(F32) + got[i][c, k].astype(F32)
-            part[c, start + k] = total.astype(BF16)
-
-        loop(0, count, add)
-        stage(kind, c, way, i + 1).start()
-
-    def both_chunk(c, way):
-        def place(j):
-            where = lax.rem(j + (1 - bit[0]) * half, replicas)
-            lines = span(rank_of(way, where), both_rows)
+        if i == 0:
+            stage(kind, c, 0, 0).wait_recv()
+        for way in range(2):
+            start = base(way, i + 1)
+            if i > 0:
+                stage(kind, c, way, i).wait_recv()
+            if i == bits - 1:
+                total = part[c, way, start].astype(F32) + got[i][c, way, 0].astype(F32)
+                if kind == "both":
+                    both_out[:, span(2 * c + way, TILE // 2)] = total.astype(BF16)
+                else:
+                    down_out[:, span(2 * c + way, piece // 2)] = total.astype(BF16)
+                continue
+
+            def add(k):
+                total = part[c, way, start + k].astype(F32) + got[i][c, way, k].astype(F32)
+                part[c, way, start + k] = total.astype(BF16)
+
+            loop(0, count, add)
+            stage(kind, c, way, i + 1).start()
+
+    def spread(kind, c, who, value):
+        part = kinds[kind][0]
+        size = value.shape[1] // 2
+        for way in range(2):
+            half_value = value[:, way * size : (way + 1) * size]
+            part[c, way, place_of(way, who)] = half_value.astype(BF16)
+
+    def both_chunk(c):
+        def place(side, j):
+            who = 2 * j + side
+            lines = span(who, both_rows)
             value = jnp.dot(x_t[lines, :], pair_d[:, span(c, TILE)], preferred_element_type=F32)
-            both_part[c, where] = value.astype(BF16)
-
-        loop(0, half, place, unroll=2)
-        stage("both", c, way, 0).start()
-        loop(half, replicas, place, unroll=2)
-
-    def down_chunk(q, way):
+            spread("both", c, who, value)
+
+        loop(0, half, functools.partial(place, 1 - bit[0]), unroll=2)
+        stage("both", c, 0, 0).start()
+        loop(0, half, functools.partial(place, bit[0]), unroll=2)
+
+    def down_chunk(q):
         cols = span(q, piece)
-        if down_rows % 16 == 0:
-
-            def place(j):
-                where = lax.rem(j + (1 - bit[0]) * half, replicas)
-                lines = span(rank_of(way, where), down_rows)
-                value = jnp.dot(h_t[lines, :], dy_all[:, cols], preferred_element_type=F32)
-                down_part[q, where] = value.astype(BF16)
-
-            loop(0, half, place, unroll=2)
-            stage("down", q, way, 0).start()
-            loop(half, replicas, place, unroll=2)
+        group = 1 if down_rows % 16 == 0 else 2
+
+        def place(side, j):
+            who = 2 * j + side
+            lines = span(who // group, group * down_rows)
+            value = jnp.dot(h_t[lines, :], dy_all[:, cols], preferred_element_type=F32)
+            for k in range(group):
+                spread("down", q, who + k, value[k * down_rows : (k + 1) * down_rows])
+
+        if group == 1:
+            loop(0, half, functools.partial(place, 1 - bit[0]), unroll=2)
+            stage("down", q, 0, 0).start()
+            loop(0, half, functools.partial(place, bit[0]), unroll=2)
         else:
-
-            def place(j):
-                lines = span(j, 2 * down_rows)
-                value = jnp.dot(h_t[lines, :], dy_all[:, cols], preferred_element_type=F32)
-                for k in range(2):
-                    some = value[k * down_rows : (k + 1) * down_rows]
-                    down_part[q, place_of(way, 2 * j + k)] = some.astype(BF16)
-
-            loop(0, half, place)
-            stage("down", q, way, 0).start()
+            loop(0, half, functools.partial(place, 0))
+            stage("down", q, 0, 0).start()
 
     last = jnp.clip(n - 1 - me, 0, n - 1)
     last_side = jnp.where(me == n - 1, 0, 1)
@@ -412,69 +412,59 @@
     def _():
         hid[...] = jnp.zeros_like(hid)
 
-    def early(k):
-        for way in range(2):
-            q = 2 * k + way
-            if way == 1:
-                combine("down", q - 1, 0, 0)
-            else:
-
-                @pl.when(k > 0)
+    def early(q):
+        @pl.when(q > 0)
+        def _():
+            combine("down", q - 1, 0)
+
+        @pl.when(is_end)
+        def _():
+            arrival(q, last_side, n - 2).wait_recv()
+            gather_hidden(last, q)
+
+            @pl.when(q == PIECES - 1)
+            def _():
+                slopes(last)
+
+        down_chunk(q)
+
+        @pl.when(q > 1)
+        def _():
+            combine("down", q - 2, 1)
+
+    loop(0, PIECES, early)
+    wide = feature // WIDE
+
+    def late(c):
+        both_chunk(c)
+
+        @pl.when(c == 0)
+        def _():
+            combine("down", PIECES - 1, 0)
+
+        @pl.when(c > 0)
+        def _():
+            combine("both", c - 1, 0)
+
+        for t in range(2):
+            j = 2 * (c - 1) + t
+
+            @pl.when(jnp.logical_and(is_end, jnp.logical_and(c > 0, j < wide)))
+            def _():
+                input_tile(last, j)
+
+                @pl.when(j == wide - 1)
                 def _():
-                    combine("down", q - 1, 1, 0)
-
-            @pl.when(is_end)
-            def _():
-                arrival(q, last_side, n - 2).wait_recv()
-                gather_hidden(last, q)
-
-            if way == 1:
-
-                @pl.when(jnp.logical_and(is_end, q == PIECES - 1))
-                def _():
-                    slopes(last)
-
-            down_chunk(q, way)
-
-    loop(0, PIECES // 2, early)
-    wide = feature // WIDE
-    share = -(-wide // (chunks - 2))
-
-    def late(k):
-        for way in range(2):
-            c = 2 * k + way
-            both_chunk(c, way)
-            if way == 1:
-                combine("both", c - 1, 0, 0)
-            else:
-
-                @pl.when(k == 0)
-                def _():
-                    combine("down", PIECES - 1, 1, 0)
-
-                @pl.when(k > 0)
-                def _():
-                    combine("both", c - 1, 1, 0)
-
-            for t in range(share):
-                j = share * (c - 2) + t
-
-                @pl.when(jnp.logical_and(is_end, jnp.logical_and(k > 0, j < wide)))
-                def _():
-                    input_tile(last, j)
-
-            @pl.when(jnp.logical_and(k > 0, k <= PIECES // 2))
-            def _():
-                combine("down", c - 2, way, 1)
-
-    loop(0, chunks // 2, late)
-    combine("both", chunks - 1, 1, 0)
-    for q in range(max(0, chunks - 2), PIECES):
-        combine("down", q, q % 2, 1)
-
-    @pl.when(is_end)
-    def _():
-        send_rows(last)
+                    send_rows(last)
+
+        for k in range(2):
+
+            @pl.when(c == 1 + 2 * k)
+            def _():
+                combine("down", PIECES - 2 + k, 1)
+
+    loop(0, chunks, late)
+    combine("both", chunks - 1, 0)
 
     for side in range(2):
         for s in range(n - 1):
@@ -511,17 +501,10 @@
 
     for i in range(1, bits - 1):
         if i > 1:
-            for way in range(2):
-                loop(0, PIECES // 2, lambda k: combine("down", 2 * k + way, way, i))
-
-        def step(k):
-            for way in range(2):
-                combine("both", 2 * k + way, way, i)
-
-        loop(0, chunks // 2, step)
-
-    for way in range(2):
-        loop(0, PIECES // 2, lambda k: combine("down", 2 * k + way, way, bits - 1))
+            loop(0, PIECES, lambda q: combine("down", q, i))
+        loop(0, chunks, lambda c: combine("both", c, i))
+
+    loop(0, PIECES, lambda q: combine("down", q, bits - 1))
 
     def takes_row(b):
         if not fold:
@@ -573,11 +556,7 @@
         picked = picked + jnp.where(ids[...] == b, comb_got[b, 0:1, :], 0.0)
     comb_grad[...] = picked
 
-    def finish(k):
-        for way in range(2):
-            combine("both", 2 * k + way, way, bits - 1)
-
-    loop(0, chunks // 2, finish)
+    loop(0, chunks, lambda c: combine("both", c, bits - 1))
 
     for target in others:
         table_copy(target).wait_send()
@@ -595,12 +574,13 @@
 
     for kind, count in (("both", chunks), ("down", PIECES)):
 
-        def drain(k):
+        def drain(c):
+            stage(kind, c, 0, 0).wait_send()
             for way in range(2):
-                for i in range(bits):
-                    stage(kind, 2 * k + way, way, i).wait_send()
-
-        loop(0, count // 2, drain)
+                for i in range(1, bits):
+                    stage(kind, c, way, i).wait_send()
+
+        loop(0, count, drain)
 
 
 def deliver_kernel(rows, comb, both, down, *refs):
@@ -677,18 +657,20 @@
         pltpu.VMEM((n, table, rows), F32),
         pltpu.VMEM((n, 8, rows), F32),
         pltpu.VMEM((n, 8, rows), F32),
-        pltpu.VMEM((chunks, replicas, both_rows, TILE), BF16),
-        pltpu.VMEM((PIECES, replicas, down_rows, piece), BF16),
+        pltpu.VMEM((chunks, 2, replicas, both_rows, TILE // 2), BF16),
+        pltpu.VMEM((PIECES, 2, replicas, down_rows, piece // 2), BF16),
     ]
     for i in range(bits):
-        scratch.append(pltpu.VMEM((chunks, replicas >> (i + 1), both_rows, TILE), BF16))
+        count = replicas >> (i + 1)
+        scratch.append(pltpu.VMEM((chunks, 2, count, both_rows, TILE // 2), BF16))
     for i in range(bits):
-        scratch.append(pltpu.VMEM((PIECES, replicas >> (i + 1), down_rows, piece), BF16))
+        count = replicas >> (i + 1)
+        scratch.append(pltpu.VMEM((PIECES, 2, count, down_rows, piece // 2), BF16))
     scratch += [pltpu.SemaphoreType.DMA((3,))]
     scratch += [pltpu.SemaphoreType.DMA((1 + PIECES, 2, n))] * 2
     scratch += [pltpu.SemaphoreType.DMA((n,))] * 6
-    scratch += [pltpu.SemaphoreType.DMA((chunks, bits))] * 2
-    scratch += [pltpu.SemaphoreType.DMA((PIECES, bits))] * 2
+    scratch += [pltpu.SemaphoreType.DMA((chunks, bits, 2))] * 2
+    scratch += [pltpu.SemaphoreType.DMA((PIECES, bits, 2))] * 2
     scratch += [pltpu.SemaphoreType.DMA((1,))] * 2
     input_grad, combine_grad, both, down = pl.pallas_call(
         functools.partial(layer_kernel, n, bits),

time: 122 us -> 118 us (0.967)
  Pallas kernels: 117 us -> 114 us
    pallas_call x1, Pallas kernels: 116 us -> 113 us  [shards(): pl.pallas_call(functools.partial(layer_kernel, n, bits), out_shape=outs,...]
where the time goes in v3:
time: 118 us
  Pallas kernels  114 us (97%)
  local copies, waits for them, and re-layouts  3.43 us (3%)
    pallas_call x1, Pallas kernels, shards(): pl.pallas_call(functools.partial(layer_kernel, n, bits), out_shape=outs,...  113 us
    unnamed x8, local copies, waits for them, and re-layouts  3.43 us

profile of v3, /device:TPU:0, one launch (start us, length us, event | category | flops | bytes accessed | tf_op | source)
XLA Modules:
  0.0 117.9 jit_solution(296858396170287834)
XLA Ops:
  0.6 0.0 copy-start
  0.6 1.0 copy-done
  1.7 0.0 copy-start.1
  1.7 1.0 copy-done.1
  2.7 0.0 copy-start.2
  2.7 0.7 copy-done.2
  3.4 0.0 copy-start.3
  3.4 0.7 copy-done.3
  4.1 112.6 %layer.1 = (bf16[128,2048]{1,0:T(8,128)(2,1)S(1)}, f32[2,128]{1,0:T(2,128)S(1)}, bf16[256,1536]{1,0:T(8,128)(2,1)S(1)}, bf16[96,2048]{1,0:T(8,128)(2,1)S(1)}) custom-call(s32[2,128]{1,0:T(2,128)S(1)} %bitcast.3, f32[2,128]{1,0:T(2,128)S(1)} %bitcast.4, bf16[128,2048]{1,0:T(8,128)(2,1)S(1)} %copy-done, bf16[128,2048]{1,0:T(8,128)(2,1)S(1)} %copy-done.1, ...), custom_call_target="tpu_custom_call" | custom-call | tf_op jit(solution)/shard_map/layer/pallas_call | solution.py:675
  116.7 1.2 %deliver.1 = (bf16[128,2048]{1,0:T(8,128)(2,1)}, f32[2,128]{1,0:T(2,128)}, bf16[1,256,768]{2,1,0:T(8,128)(2,1)}, bf16[1,256,768]{2,1,0:T(8,128)(2,1)}, bf16[1,96,2048]{2,1,0:T(8,128)(2,1)}) custom-call(bf16[128,2048]{1,0:T(8,128)(2,1)S(1)} %get-tuple-element.14.rows, f32[2,128]{1,0:T(2,128)S(1)} %get-tuple-element.15.comb, ...), custom_call_target="tpu_custom_call" | custom-call | tf_op jit(solution)/shard_map/deliver/pallas_call | solution.py:612
Async XLA Ops:
  0.6 1.0 copy-start
  1.7 1.0 copy-start.1
  2.7 0.7 copy-start.2
  3.4 0.7 copy-start.3

commit v4 on v3

--- a/solution.py
+++ b/solution.py
@@ -46,12 +46,12 @@
     in_grad, comb_grad, both_out, down_out = refs[7:11]
     x_all, dy_all, x_t, wg, wu, wd, slope, act_all = refs[11:19]
     h_all, h_t, pair_d, hid, rows_out, rows_got = refs[19:25]
-    tables, comb_out, comb_got = refs[25:28]
-    both_part, down_part = refs[28:30]
-    both_got, down_got = refs[30 : 30 + bits], refs[30 + bits : 30 + 2 * bits]
-    rest = refs[30 + 2 * bits :]
+    tables, comb_out, comb_got, h_guest, down_guest = refs[25:30]
+    both_part, down_part = refs[30:32]
+    both_got, down_got = refs[32 : 32 + bits], refs[32 + bits : 32 + 2 * bits]
+    rest = refs[32 + 2 * bits :]
     load, a_send, a_recv, t_send, t_recv, r_send, r_recv, c_send, c_recv = rest[:9]
-    b_send, b_recv, d_send, d_recv, f_send, f_recv = rest[9:15]
+    b_send, b_recv, d_send, d_recv, f_send, f_recv, h_send, h_recv = rest[9:17]
 
     me = lax.axis_index("expert")
     rank = lax.axis_index("dp")
@@ -141,10 +141,43 @@
             target,
         )
 
+    def tile_copy(target, j):
+        cols = span(j, WIDE)
+        return remote(
+            rows_out.at[target, :, cols],
+            rows_got.at[me, :, cols],
+            r_send.at[target],
+            r_recv.at[me],
+            "expert",
+            target,
+        )
+
     fold = n == 4
     ally = n - 1 - me
     near = jnp.where(2 * me < n, 0, n - 1)
     far = n - 1 - near
+
+    shared = PIECES - 1 if fold else PIECES
+    helper = jnp.where(me == 0, 1, n - 2)
+    own_down = PIECES
+    if fold:
+        own_down = jnp.where(is_end, shared, PIECES + 1)
+
+    def hidden_copy(b):
+        cols = span(b, rows)
+        return remote(
+            h_t.at[:, cols], h_guest.at[:, cols], h_send.at[b], h_recv.at[b], "expert", helper
+        )
+
+    def guest_copy():
+        return remote(
+            down_guest,
+            down_out.at[:, span(PIECES - 1, piece)],
+            f_send.at[1],
+            f_recv.at[1],
+            "expert",
+            near,
+        )
 
     def fold_copy():
         return remote(
@@ -171,8 +204,11 @@
         table_copy(target).start()
     for p in [None] + list(range(PIECES)):
         for side in range(2):
-
-            @pl.when(sends(side, 0))
+            ready = sends(side, 0)
+            if p is not None and p > 0:
+                ready = jnp.logical_and(ready, me == (0, n - 1)[side])
+
+            @pl.when(ready)
             def _():
                 hop(p, side, 0, True).start()
 
@@ -208,21 +244,27 @@
             cols = span(j, TILE)
             x_t[cols, own] = x_all[own, cols].T
 
+        if fold:
+
+            @pl.when(is_end)
+            def _():
+                hidden_copy(b).start()
+
         loop(0, feature // TILE, turn)
 
-    def gather_hidden(b, q):
+    def gather_hidden(b, q, slot=0):
         cols = span(q, piece)
-        hid[...] += lax.dot_general(
+        hid[slot] += lax.dot_general(
             dy_all[span(b, rows), cols], wd[:, cols], LAST, preferred_element_type=F32
         )
 
-    def slopes(b):
+    def slopes(b, slot=0):
         own = span(b, rows)
         coef = coefficient(b)
 
         def tile(j, total):
             cols = span(j, TILE)
-            grad = hid[:, cols]
+            grad = hid[slot, :, cols]
             total = total + jnp.sum(h_all[own, cols].astype(F32) * grad, axis=1, keepdims=True)
             grad = coef * grad
             pair_d[own, cols] = (grad * slope[own, cols]).astype(BF16)
@@ -245,18 +287,34 @@
         row_copy(b).start()
         comb_copy(b).start()
 
+    def first(d):
+        return jnp.where(jnp.logical_or(d == 0, me >= d), 0, 1)
+
+    def bound(d):
+        return jnp.where(jnp.logical_and(d > 0, me + d < n), 2, 1)
+
+    def source(side, d):
+        return jnp.clip(me + d * (2 * side - 1), 0, n - 1)
+
+    def by_end(side):
+        return jnp.where(side == 0, me == n - 2, me == 1)
+
+    def back(b, d):
+        hid[0] = jnp.zeros(hid.shape[1:], F32)
+        loop(0, PIECES, lambda q: gather_hidden(b, q))
+        slopes(b)
+        loop(0, feature // WIDE, functools.partial(input_tile, b))
+
+        @pl.when(jnp.logical_and(is_end, d > 0))
+        def _():
+            send_rows(b)
+
     def distance(d):
-        low = jnp.where(jnp.logical_or(d == 0, me >= d), 0, 1)
-        high = jnp.where(jnp.logical_and(d > 0, me + d < n), 2, 1)
-
-        def source(side):
-            return jnp.clip(me + d * (2 * side - 1), 0, n - 1)
-
         def take(side):
             @pl.when(d > 0)
             def _():
                 arrival(None, side, d - 1).wait_recv()
-                b = source(side)
+                b = source(side, d)
                 remote(
                     tables.at[b], tables.at[b], t_send.at[b], t_recv.at[b], "expert", me
                 ).wait_recv()
@@ -265,37 +323,46 @@
                 def _():
                     hop(None, side, d).start()
 
-        loop(low, high, take)
-        loop(low, high, lambda side: forward(source(side)))
-
-        def back(side):
-            b = source(side)
-            hid[...] = jnp.zeros_like(hid)
-
-            def part(q):
-                @pl.when(d > 0)
+                    @pl.when(d == 1)
+                    def _():
+                        for p in range(1, PIECES):
+                            hop(p, side, 0, True).start()
+
+        loop(first(d), bound(d), take)
+        loop(first(d), bound(d), lambda side: forward(source(side, d)))
+        e = jnp.maximum(d - 1, 0)
+
+        def take_piece(i):
+            q, side = i // 2, lax.rem(i, 2)
+            here = jnp.logical_and(side >= first(e), side < bound(e))
+
+            @pl.when(jnp.logical_and(here, e > 0))
+            def _():
+                arrival(q, side, e - 1).wait_recv()
+                later = jnp.logical_and(by_end(side), e == n - 3)
+
+                @pl.when(jnp.logical_and(passes(side), jnp.logical_not(later)))
                 def _():
-                    arrival(q, side, d - 1).wait_recv()
-
-                    @pl.when(passes(side))
-                    def _():
-                        hop(q, side, d).start()
-
-                gather_hidden(b, q)
-
-            loop(0, PIECES, part)
-            slopes(b)
-            loop(0, feature // WIDE, functools.partial(input_tile, b))
-
-            @pl.when(jnp.logical_and(is_end, d > 0))
-            def _():
-                send_rows(b)
-
-        @pl.when(d < n - 1)
-        def _():
-            loop(low, high, back)
+                    hop(q, side, e).start()
+
+        @pl.when(jnp.logical_or(d == 0, jnp.logical_and(d > 1, d < n - 1)))
+        def _():
+            loop(0, 2 * PIECES, take_piece)
+            loop(first(e), bound(e), lambda side: back(source(side, e), e))
 
     loop(0, n, distance)
+
+    @pl.when(jnp.logical_or(me == 1, me == n - 2))
+    def _():
+        side = jnp.where(me == 1, 1, 0)
+
+        def take(q):
+            arrival(q, side, n - 3).wait_recv()
+            hop(q, side, n - 3).start()
+            hop(q, side, n - 2).start()
+
+        loop(0, PIECES, take)
+        back(source(side, n - 2), n - 2)
 
     if fold:
 
@@ -357,6 +424,16 @@
                 total = part[c, way, start].astype(F32) + got[i][c, way, 0].astype(F32)
                 if kind == "both":
                     both_out[:, span(2 * c + way, TILE // 2)] = total.astype(BF16)
+                elif fold:
+
+                    @pl.when(c < PIECES)
+                    def _():
+                        down_out[:, span(2 * c + way, piece // 2)] = total.astype(BF16)
+
+                    @pl.when(c == PIECES)
+                    def _():
+                        down_guest[:, span(way, piece // 2)] = total.astype(BF16)
+
                 else:
                     down_out[:, span(2 * c + way, piece // 2)] = total.astype(BF16)
                 continue
@@ -386,14 +463,14 @@
         stage("both", c, 0, 0).start()
         loop(0, half, functools.partial(place, bit[0]), unroll=2)
 
-    def down_chunk(q):
-        cols = span(q, piece)
+    def down_chunk(q, held=h_t):
+        cols = span(min(q, PIECES - 1) if isinstance(q, int) else q, piece)
         group = 1 if down_rows % 16 == 0 else 2
 
         def place(side, j):
             who = 2 * j + side
             lines = span(who // group, group * down_rows)
-            value = jnp.dot(h_t[lines, :], dy_all[:, cols], preferred_element_type=F32)
+            value = jnp.dot(held[lines, :], dy_all[:, cols], preferred_element_type=F32)
             for k in range(group):
                 spread("down", q, who + k, value[k * down_rows : (k + 1) * down_rows])
 
@@ -406,105 +483,148 @@
             stage("down", q, 0, 0).start()
 
     last = jnp.clip(n - 1 - me, 0, n - 1)
+    prior = jnp.where(me == n - 1, 1, n - 2)
     last_side = jnp.where(me == n - 1, 0, 1)
 
     @pl.when(is_end)
     def _():
         hid[...] = jnp.zeros_like(hid)
 
+    wide = feature // WIDE
+
+    def last_tile(j):
+        @pl.when(jnp.logical_and(is_end, j < 2 * wide))
+        def _():
+            b = jnp.where(j < wide, last, prior)
+            tile = lax.rem(j, wide)
+            input_tile(b, tile)
+            tile_copy(b, tile).start()
+
+            @pl.when(tile == wide - 1)
+            def _():
+                comb_copy(b).start()
+
     def early(q):
+        @pl.when(is_end)
+        def _():
+            for slot, b in enumerate((prior, last)):
+                arrival(q, last_side, n - 3 + slot).wait_recv()
+                gather_hidden(b, q, slot)
+
+        down_chunk(q)
+        combine("down", q, 0)
+
         @pl.when(q > 0)
         def _():
-            combine("down", q - 1, 0)
-
-        @pl.when(is_end)
-        def _():
-            arrival(q, last_side, n - 2).wait_recv()
-            gather_hidden(last, q)
-
-            @pl.when(q == PIECES - 1)
+            combine("down", q - 1, 1)
+
+    loop(0, PIECES - 1, early)
+
+    @pl.when(is_end)
+    def _():
+        for slot, b in enumerate((prior, last)):
+            arrival(PIECES - 1, last_side, n - 3 + slot).wait_recv()
+            gather_hidden(b, PIECES - 1, slot)
+            slopes(b, slot)
+
+    if fold:
+
+        @pl.when(is_mid)
+        def _():
+            for b in range(n):
+                cols = span(b, rows)
+                slot = h_guest.at[:, cols]
+                remote(slot, slot, h_send.at[b], h_recv.at[b], "expert", me).wait_recv()
+            down_chunk(PIECES, h_guest)
+
+    both_chunk(0)
+    both_chunk(1)
+    combine("both", 0, 0)
+    combine("down", PIECES - 2, 1)
+    last_tile(0)
+    combine("both", 1, 0)
+
+    def rest_down(i):
+        if i == 0:
+            down_chunk(PIECES - 1)
+            if fold:
+                combine("down", PIECES, 0)
+        combine("down", PIECES - 1, i)
+        if fold and i > 0:
+            combine("down", PIECES, i)
+
+    def when_owned(body):
+        if fold:
+            pl.when(is_mid)(body)
+        else:
+            body()
+
+    when_owned(lambda: rest_down(0))
+    last_tile(1)
+    last_tile(2)
+
+    def settle():
+        for side in range(2):
+            for s in range(n - 1):
+
+                @pl.when(sends(side, s))
+                def _():
+                    hop(None, side, s).wait_send()
+                    for p in range(PIECES):
+                        hop(p, side, s).wait_send()
+
+        if fold:
+
+            @pl.when(is_mid)
             def _():
-                slopes(last)
-
-        down_chunk(q)
-
-        @pl.when(q > 1)
-        def _():
-            combine("down", q - 2, 1)
-
-    loop(0, PIECES, early)
-    wide = feature // WIDE
+                folded().wait_recv()
+
+                def add(j):
+                    cols = span(j, TILE)
+                    total = rows_out[near, :, cols].astype(F32) + rows_got[me, :, cols].astype(F32)
+                    rows_out[near, :, cols] = total.astype(BF16)
+
+                loop(0, feature // TILE, add)
+                row_copy(near).start()
+                comb_copy(near).start()
+                comb_copy(far).start()
+
+        else:
+            for target in others:
+                outer = jnp.logical_or(target == 0, target == n - 1)
+
+                @pl.when(jnp.logical_and(is_mid, outer))
+                def _():
+                    send_rows(target)
 
     def late(c):
         both_chunk(c)
-
-        @pl.when(c == 0)
-        def _():
-            combine("down", PIECES - 1, 0)
-
-        @pl.when(c > 0)
-        def _():
-            combine("both", c - 1, 0)
-
         for t in range(2):
-            j = 2 * (c - 1) + t
-
-            @pl.when(jnp.logical_and(is_end, jnp.logical_and(c > 0, j < wide)))
-            def _():
-                input_tile(last, j)
-
-                @pl.when(j == wide - 1)
-                def _():
-                    send_rows(last)
-
-        for k in range(2):
-
-            @pl.when(c == 1 + 2 * k)
-            def _():
-                combine("down", PIECES - 2 + k, 1)
-
-    loop(0, chunks, late)
-    combine("both", chunks - 1, 0)
-
-    for side in range(2):
-        for s in range(n - 1):
-
-            @pl.when(sends(side, s))
-            def _():
-                hop(None, side, s).wait_send()
-                for p in range(PIECES):
-                    hop(p, side, s).wait_send()
-
-    if fold:
-
-        @pl.when(is_mid)
-        def _():
-            folded().wait_recv()
-
-            def add(j):
-                cols = span(j, TILE)
-                total = rows_out[near, :, cols].astype(F32) + rows_got[me, :, cols].astype(F32)
-                rows_out[near, :, cols] = total.astype(BF16)
-
-            loop(0, feature // TILE, add)
-            row_copy(near).start()
-            comb_copy(near).start()
-            comb_copy(far).start()
-
-    else:
-        for target in others:
-            outer = jnp.logical_or(target == 0, target == n - 1)
-
-            @pl.when(jnp.logical_and(is_mid, outer))
-            def _():
-                send_rows(target)
+            last_tile(2 * c - 1 + t)
+        combine("both", c, 0)
+
+        @pl.when(c == 3)
+        def _():
+            when_owned(lambda: rest_down(1))
+
+        @pl.when(c == 2)
+        def _():
+            settle()
+
+    loop(2, chunks, late)
 
     for i in range(1, bits - 1):
         if i > 1:
-            loop(0, PIECES, lambda q: combine("down", q, i))
+            loop(0, own_down, lambda q: combine("down", q, i))
         loop(0, chunks, lambda c: combine("both", c, i))
 
-    loop(0, PIECES, lambda q: combine("down", q, bits - 1))
+    loop(0, own_down, lambda q: combine("down", q, bits - 1))
+    if fold:
+
+        @pl.when(is_mid)
+        def _():
+            guest_copy().start()
+
 
     def takes_row(b):
         if not fold:
@@ -558,6 +678,19 @@
 
     loop(0, chunks, lambda c: combine("both", c, bits - 1))
 
+    if fold:
+
+        @pl.when(is_end)
+        def _():
+            slot = down_out.at[:, span(PIECES - 1, piece)]
+            remote(slot, slot, f_send.at[1], f_recv.at[1], "expert", me).wait_recv()
+            for b in range(n):
+                hidden_copy(b).wait_send()
+
+        @pl.when(is_mid)
+        def _():
+            guest_copy().wait_send()
+
     for target in others:
         table_copy(target).wait_send()
         comb_copy(target).wait_send()
@@ -572,7 +705,7 @@
         def _():
             fold_copy().wait_send()
 
-    for kind, count in (("both", chunks), ("down", PIECES)):
+    for kind, count in (("both", chunks), ("down", own_down)):
 
         def drain(c):
             stage(kind, c, 0, 0).wait_send()
@@ -651,27 +784,30 @@
         pltpu.VMEM((everyone, width), BF16),
         pltpu.VMEM((width, everyone), BF16),
         pltpu.VMEM((everyone, 2 * width), BF16),
-        pltpu.VMEM((rows, width), F32),
+        pltpu.VMEM((2, rows, width), F32),
         pltpu.VMEM((n, rows, feature), BF16),
         pltpu.VMEM((n, rows, feature), BF16),
         pltpu.VMEM((n, table, rows), F32),
         pltpu.VMEM((n, 8, rows), F32),
         pltpu.VMEM((n, 8, rows), F32),
+        pltpu.VMEM((width, everyone), BF16),
+        pltpu.VMEM((down_rows, piece), BF16),
         pltpu.VMEM((chunks, 2, replicas, both_rows, TILE // 2), BF16),
-        pltpu.VMEM((PIECES, 2, replicas, down_rows, piece // 2), BF16),
+        pltpu.VMEM((PIECES + 1, 2, replicas, down_rows, piece // 2), BF16),
     ]
     for i in range(bits):
         count = replicas >> (i + 1)
         scratch.append(pltpu.VMEM((chunks, 2, count, both_rows, TILE // 2), BF16))
     for i in range(bits):
         count = replicas >> (i + 1)
-        scratch.append(pltpu.VMEM((PIECES, 2, count, down_rows, piece // 2), BF16))
+        scratch.append(pltpu.VMEM((PIECES + 1, 2, count, down_rows, piece // 2), BF16))
     scratch += [pltpu.SemaphoreType.DMA((3,))]
     scratch += [pltpu.SemaphoreType.DMA((1 + PIECES, 2, n))] * 2
     scratch += [pltpu.SemaphoreType.DMA((n,))] * 6
     scratch += [pltpu.SemaphoreType.DMA((chunks, bits, 2))] * 2
-    scratch += [pltpu.SemaphoreType.DMA((PIECES, bits, 2))] * 2
-    scratch += [pltpu.SemaphoreType.DMA((1,))] * 2
+    scratch += [pltpu.SemaphoreType.DMA((PIECES + 1, bits, 2))] * 2
+    scratch += [pltpu.SemaphoreType.DMA((2,))] * 2
+    scratch += [pltpu.SemaphoreType.DMA((n,))] * 2
     input_grad, combine_grad, both, down = pl.pallas_call(
         functools.partial(layer_kernel, n, bits),
         out_shape=outs,

time: 118 us -> 114 us (0.966)
  Pallas kernels: 114 us -> 110 us
    pallas_call x1, Pallas kernels: 113 us -> 109 us  [shards(): pl.pallas_call(functools.partial(layer_kernel, n, bits), out_shape=outs,...]
where the time goes in v4:
time: 114 us
  Pallas kernels  110 us (96%)
  local copies, waits for them, and re-layouts  3.43 us (3%)
    pallas_call x1, Pallas kernels, shards(): pl.pallas_call(functools.partial(layer_kernel, n, bits), out_shape=outs,...  109 us
    unnamed x8, local copies, waits for them, and re-layouts  3.43 us

profile of v4, /device:TPU:0, one launch (start us, length us, event | category | flops | bytes accessed | tf_op | source)
XLA Modules:
  0.0 113.9 jit_solution(14789577625468083795)
XLA Ops:
  0.6 0.0 copy-start
  0.6 1.0 copy-done
  1.7 0.0 copy-start.1
  1.7 1.0 copy-done.1
  2.7 0.0 copy-start.2
  2.7 0.7 copy-done.2
  3.4 0.0 copy-start.3
  3.4 0.7 copy-done.3
  4.1 108.5 %layer.1 = (bf16[128,2048]{1,0:T(8,128)(2,1)S(1)}, f32[2,128]{1,0:T(2,128)S(1)}, bf16[256,1536]{1,0:T(8,128)(2,1)S(1)}, bf16[96,2048]{1,0:T(8,128)(2,1)S(1)}) custom-call(s32[2,128]{1,0:T(2,128)S(1)} %bitcast.3, f32[2,128]{1,0:T(2,128)S(1)} %bitcast.4, bf16[128,2048]{1,0:T(8,128)(2,1)S(1)} %copy-done, bf16[128,2048]{1,0:T(8,128)(2,1)S(1)} %copy-done.1, ...), custom_call_target="tpu_custom_call" | custom-call | tf_op jit(solution)/shard_map/layer/pallas_call | solution.py:811
  112.6 1.2 %deliver.1 = (bf16[128,2048]{1,0:T(8,128)(2,1)}, f32[2,128]{1,0:T(2,128)}, bf16[1,256,768]{2,1,0:T(8,128)(2,1)}, bf16[1,256,768]{2,1,0:T(8,128)(2,1)}, bf16[1,96,2048]{2,1,0:T(8,128)(2,1)}) custom-call(bf16[128,2048]{1,0:T(8,128)(2,1)S(1)} %get-tuple-element.14.rows, f32[2,128]{1,0:T(2,128)S(1)} %get-tuple-element.15.comb, ...), custom_call_target="tpu_custom_call" | custom-call | tf_op jit(solution)/shard_map/deliver/pallas_call | solution.py:745
Async XLA Ops:
  0.6 1.0 copy-start
  1.7 1.0 copy-start.1
  2.7 0.7 copy-start.2
  3.4 0.7 copy-start.3

commit v5 on v4

--- a/solution.py
+++ b/solution.py
@@ -42,7 +42,11 @@
 
 
 def layer_kernel(n, bits, *refs):
-    ids, comb, x_in, dy_in, g_in, u_in, d_in = refs[:7]
+    routes, both_in, g_in, u_in, d_in = refs[:5]
+    top = routes.shape[0] // 2
+    ids, comb = routes.at[:top], routes.at[top:]
+    x_in, dy_in = both_in.at[0], both_in.at[1]
+    refs = (None, None) + refs
     in_grad, comb_grad, both_out, down_out = refs[7:11]
     x_all, dy_all, x_t, wg, wu, wd, slope, act_all = refs[11:19]
     h_all, h_t, pair_d, hid, rows_out, rows_got = refs[19:25]
@@ -88,9 +92,9 @@
     for b in range(bits):
         pl.semaphore_signal(barrier, inc=1, device_id={"dp": mate[b]}, device_id_type=MESH)
 
-    expert = lax.broadcasted_iota(jnp.int32, tables.shape[1:], 0)
+    expert = lax.broadcasted_iota(jnp.int32, tables.shape[1:], 0).astype(F32)
     weight = jnp.where(expert == ids[0:1, :], comb[0:1, :], 0.0)
-    for k in range(1, ids.shape[0]):
+    for k in range(1, top):
         weight = weight + jnp.where(expert == ids[k : k + 1, :], comb[k : k + 1, :], 0.0)
     tables[me] = weight
 
@@ -104,19 +108,24 @@
 
     def hop(p, side, s, own=False):
         step = 1 - 2 * side
-        slot = view(p, jnp.clip(me - step * s, 0, n - 1))
+        block = jnp.clip(me - step * s, 0, n - 1)
+        slot = view(p, block)
         target = jnp.clip(me + step, 0, n - 1)
         i = index(p)
         src = slot
         if own:
             src = x_in if p is None else dy_in.at[:, span(p, piece)]
-        return remote(src, slot, a_send.at[i, side, s], a_recv.at[i, side, s], "expert", target)
+        return remote(src, slot, a_send.at[side, s], a_recv.at[i, block], "expert", target)
 
     def arrival(p, side, s):
         step = 1 - 2 * side
-        slot = view(p, jnp.clip(me - step * (s + 1), 0, n - 1))
-        i = index(p)
-        return remote(slot, slot, a_send.at[i, side, s], a_recv.at[i, side, s], "expert", me)
+        block = jnp.clip(me - step * (s + 1), 0, n - 1)
+        slot = view(p, block)
+        return remote(slot, slot, a_send.at[side, s], a_recv.at[index(p), block], "expert", me)
+
+    def hops(side, s):
+        slot = x_all.at[pl.ds(0, 2 * rows)]
+        return remote(slot, slot, a_send.at[side, s], a_recv.at[0, 0], "expert", me)
 
     def sends(side, s):
         if side == 0:
@@ -128,7 +137,7 @@
 
     def table_copy(target):
         return remote(
-            tables.at[me], tables.at[me], t_send.at[target], t_recv.at[me], "expert", target
+            tables.at[me], tables.at[me], t_send.at[0], t_recv.at[me], "expert", target
         )
 
     def row_copy(target):
@@ -166,7 +175,7 @@
     def hidden_copy(b):
         cols = span(b, rows)
         return remote(
-            h_t.at[:, cols], h_guest.at[:, cols], h_send.at[b], h_recv.at[b], "expert", helper
+            h_t.at[:, cols], h_guest.at[:, cols], h_send.at[0], h_recv.at[0], "expert", helper
         )
 
     def guest_copy():
@@ -192,11 +201,15 @@
         return remote(
             comb_out.at[target],
             comb_got.at[me],
-            c_send.at[target],
-            c_recv.at[me],
+            c_send.at[0],
+            c_recv.at[0],
             "expert",
             target,
         )
+
+    def few(ref, send, recv):
+        slot = ref.at[pl.ds(0, n - 1)]
+        return remote(slot, slot, send.at[0], recv.at[0], "expert", me)
 
     pl.semaphore_wait(barrier, n - 1 + bits)
     others = [lax.rem(me + k, n) for k in range(1, n)]
@@ -316,7 +329,7 @@
                 arrival(None, side, d - 1).wait_recv()
                 b = source(side, d)
                 remote(
-                    tables.at[b], tables.at[b], t_send.at[b], t_recv.at[b], "expert", me
+                    tables.at[b], tables.at[b], t_send.at[0], t_recv.at[b], "expert", me
                 ).wait_recv()
 
                 @pl.when(passes(side))
@@ -405,21 +418,25 @@
         return remote(
             part.at[c, pick, pl.ds(start, count)],
             got[i].at[c, pick],
-            send.at[c, i, way],
-            recv.at[c, i, way],
+            send.at[c],
+            recv.at[c, i],
             "dp",
             mate[b],
         )
+
+    def staged(kind, c):
+        part, _, send, recv = kinds[kind]
+        slot = part.at[c, :, pl.ds(0, replicas - 1)]
+        return remote(slot, slot, send.at[c], recv.at[c, 0], "dp", rank)
 
     def combine(kind, c, i):
         part, got, _, _ = kinds[kind]
         count = replicas >> (i + 1)
-        if i == 0:
-            stage(kind, c, 0, 0).wait_recv()
+        recv = kinds[kind][3]
+        slot = got[i].at[c]
+        remote(slot, slot, kinds[kind][2].at[c], recv.at[c, i], "dp", rank).wait_recv()
         for way in range(2):
             start = base(way, i + 1)
-            if i > 0:
-                stage(kind, c, way, i).wait_recv()
             if i == bits - 1:
                 total = part[c, way, start].astype(F32) + got[i][c, way, 0].astype(F32)
                 if kind == "both":
@@ -531,10 +548,7 @@
 
         @pl.when(is_mid)
         def _():
-            for b in range(n):
-                cols = span(b, rows)
-                slot = h_guest.at[:, cols]
-                remote(slot, slot, h_send.at[b], h_recv.at[b], "expert", me).wait_recv()
+            remote(h_guest, h_guest, h_send.at[0], h_recv.at[0], "expert", me).wait_recv()
             down_chunk(PIECES, h_guest)
 
     both_chunk(0)
@@ -569,9 +583,7 @@
 
                 @pl.when(sends(side, s))
                 def _():
-                    hop(None, side, s).wait_send()
-                    for p in range(PIECES):
-                        hop(p, side, s).wait_send()
+                    hops(side, s).wait_send()
 
         if fold:
 
@@ -644,9 +656,8 @@
                 rows_got.at[b], rows_got.at[b], r_send.at[b], r_recv.at[b], "expert", me
             ).wait_recv()
 
-        remote(
-            comb_got.at[b], comb_got.at[b], c_send.at[b], c_recv.at[b], "expert", me
-        ).wait_recv()
+
+    few(comb_got, c_send, c_recv).wait_recv()
 
     def total_rows(who):
         def tile(j):
@@ -671,12 +682,10 @@
     else:
         total_rows(others)
 
-    picked = jnp.where(ids[...] == me, comb_out[me, 0:1, :], 0.0)
+    picked = jnp.where(ids[...] == me.astype(F32), comb_out[me, 0:1, :], 0.0)
     for b in others:
-        picked = picked + jnp.where(ids[...] == b, comb_got[b, 0:1, :], 0.0)
+        picked = picked + jnp.where(ids[...] == b.astype(F32), comb_got[b, 0:1, :], 0.0)
     comb_grad[...] = picked
-
-    loop(0, chunks, lambda c: combine("both", c, bits - 1))
 
     if fold:
 
@@ -684,16 +693,15 @@
         def _():
             slot = down_out.at[:, span(PIECES - 1, piece)]
             remote(slot, slot, f_send.at[1], f_recv.at[1], "expert", me).wait_recv()
-            for b in range(n):
-                hidden_copy(b).wait_send()
+            remote(h_t, h_t, h_send.at[0], h_recv.at[0], "expert", me).wait_send()
 
         @pl.when(is_mid)
         def _():
             guest_copy().wait_send()
 
+    few(tables, t_send, t_recv).wait_send()
+    few(comb_out, c_send, c_recv).wait_send()
     for target in others:
-        table_copy(target).wait_send()
-        comb_copy(target).wait_send()
 
         @pl.when(gives_row(target))
         def _():
@@ -705,15 +713,13 @@
         def _():
             fold_copy().wait_send()
 
-    for kind, count in (("both", chunks), ("down", own_down)):
-
-        def drain(c):
-            stage(kind, c, 0, 0).wait_send()
-            for way in range(2):
-                for i in range(1, bits):
-                    stage(kind, c, way, i).wait_send()
-
-        loop(0, count, drain)
+    loop(0, own_down, lambda q: staged("down", q).wait_send())
+
+    def finish(c):
+        combine("both", c, bits - 1)
+        staged("both", c).wait_send()
+
+    loop(0, chunks, finish)
 
 
 def deliver_kernel(rows, comb, both, down, *refs):
@@ -802,23 +808,24 @@
         count = replicas >> (i + 1)
         scratch.append(pltpu.VMEM((PIECES + 1, 2, count, down_rows, piece // 2), BF16))
     scratch += [pltpu.SemaphoreType.DMA((3,))]
-    scratch += [pltpu.SemaphoreType.DMA((1 + PIECES, 2, n))] * 2
-    scratch += [pltpu.SemaphoreType.DMA((n,))] * 6
-    scratch += [pltpu.SemaphoreType.DMA((chunks, bits, 2))] * 2
-    scratch += [pltpu.SemaphoreType.DMA((PIECES + 1, bits, 2))] * 2
+    for shape in ((2, n - 1), (1 + PIECES, n), (1,), (n,), (n,), (n,), (1,), (1,)):
+        scratch.append(pltpu.SemaphoreType.DMA(shape))
+    for count in (chunks, PIECES + 1):
+        scratch += [pltpu.SemaphoreType.DMA((count,)), pltpu.SemaphoreType.DMA((count, bits))]
     scratch += [pltpu.SemaphoreType.DMA((2,))] * 2
-    scratch += [pltpu.SemaphoreType.DMA((n,))] * 2
+    scratch += [pltpu.SemaphoreType.DMA((1,))] * 2
+    routes = jnp.concatenate([expert_ids.T.astype(F32), combine.T])
     input_grad, combine_grad, both, down = pl.pallas_call(
         functools.partial(layer_kernel, n, bits),
         out_shape=outs,
-        in_specs=[VMEM] * 4 + [HBM] * 3,
+        in_specs=[VMEM] * 2 + [HBM] * 3,
         out_specs=[VMEM] * 4,
         scratch_shapes=scratch,
         compiler_params=pltpu.CompilerParams(
             collective_id=0, has_side_effects=True, vmem_limit_bytes=LIMIT
         ),
         name="layer",
-    )(expert_ids.T, combine.T, tokens, cotangent, w_gate, w_up, w_down)
+    )(routes, jnp.stack([tokens, cotangent]), w_gate, w_up, w_down)
     return deliver(input_grad, combine_grad, both, down)
 
 

time: 114 us -> 112 us (0.982)
  local copies, waits for them, and re-layouts: 3.43 us -> 0 us
  other arithmetic: 0 us -> 2.66 us
  Pallas kernels: 110 us -> 108 us
    unnamed x8 -> x0, local copies, waits for them, and re-layouts: 3.43 us -> none
    pallas_call x1, Pallas kernels: 109 us -> 107 us  [shards(): pl.pallas_call(functools.partial(layer_kernel, n, bits), out_shape=outs,...]
    another operation x0 -> x1, other arithmetic: none -> 1.3 us  [shards(): jnp.stack([tokens, cotangent])]
where the time goes in v5:
time: 112 us
  Pallas kernels  108 us (96%)
  other arithmetic  2.66 us (2%)
    pallas_call x1, Pallas kernels, shards(): pl.pallas_call(functools.partial(layer_kernel, n, bits), out_shape=outs,...  107 us

profile of v5, /device:TPU:0, one launch (start us, length us, event | category | flops | bytes accessed | tf_op | source)
XLA Modules:
  0.0 111.6 jit_solution(8021410131208115591)
XLA Ops:
  0.6 0.7 convert_bitcast_fusion
  1.3 0.7 pad_maximum_fusion.1.refs_0_
  2.0 1.3 %pad_maximum_fusion.refs_1_ = bf16[2,128,2048]{2,1,0:T(8,128)(2,1)S(1)} fusion(bf16[1,128,2048]{2,1,0:T(8,128)(2,1)} %bitcast.6, bf16[1,128,2048]{2,1,0:T(8,128)(2,1)} %bitcast.7), kind=kLoop, calls=%fused_computation | loop fusion | flops 524288 | bytes 2097152 | tf_op jit(solution)/shard_map/stack | solution.py:828
  3.3 107.1 %layer.1 = (bf16[128,2048]{1,0:T(8,128)(2,1)S(1)}, f32[2,128]{1,0:T(2,128)S(1)}, bf16[256,1536]{1,0:T(8,128)(2,1)S(1)}, bf16[96,2048]{1,0:T(8,128)(2,1)S(1)}) custom-call(f32[4,128]{1,0:T(4,128)S(1)} %pad_maximum_fusion.1.refs_0_, bf16[2,128,2048]{2,1,0:T(8,128)(2,1)S(1)} %pad_maximum_fusion.refs_1_, bf16[1,2048,768]{2,1,0:T(8,128)(2,1)} %refs_2_.1, ...), custom_call_target="tpu_custom_call" | custom-call | tf_op jit(solution)/shard_map/layer/pallas_call | solution.py:818
  110.4 1.2 %deliver.1 = (bf16[128,2048]{1,0:T(8,128)(2,1)}, f32[2,128]{1,0:T(2,128)}, bf16[1,256,768]{2,1,0:T(8,128)(2,1)}, bf16[1,256,768]{2,1,0:T(8,128)(2,1)}, bf16[1,96,2048]{2,1,0:T(8,128)(2,1)}) custom-call(bf16[128,2048]{1,0:T(8,128)(2,1)S(1)} %get-tuple-element.14.rows, f32[2,128]{1,0:T(2,128)S(1)} %get-tuple-element.15.comb, ...), custom_call_target="tpu_custom_call" | custom-call | tf_op jit(solution)/shard_map/deliver/pallas_call | solution.py:751

commit v6 on v5

--- a/solution.py
+++ b/solution.py
@@ -43,8 +43,7 @@
 
 def layer_kernel(n, bits, *refs):
     routes, both_in, g_in, u_in, d_in = refs[:5]
-    top = routes.shape[0] // 2
-    ids, comb = routes.at[:top], routes.at[top:]
+    top = routes.shape[1]
     x_in, dy_in = both_in.at[0], both_in.at[1]
     refs = (None, None) + refs
     in_grad, comb_grad, both_out, down_out = refs[7:11]
@@ -92,10 +91,9 @@
     for b in range(bits):
         pl.semaphore_signal(barrier, inc=1, device_id={"dp": mate[b]}, device_id_type=MESH)
 
-    expert = lax.broadcasted_iota(jnp.int32, tables.shape[1:], 0).astype(F32)
-    weight = jnp.where(expert == ids[0:1, :], comb[0:1, :], 0.0)
+    weight = routes[1, 0]
     for k in range(1, top):
-        weight = weight + jnp.where(expert == ids[k : k + 1, :], comb[k : k + 1, :], 0.0)
+        weight = weight + routes[1, k]
     tables[me] = weight
 
     def view(p, block):
@@ -251,7 +249,7 @@
             h_all[own, cols] = hidden
             h_t[cols, own] = (coef * hidden.astype(F32)).T.astype(BF16)
 
-        loop(0, width // TILE, tile)
+        loop(0, width // TILE, tile, unroll=True)
 
         def turn(j):
             cols = span(j, TILE)
@@ -284,7 +282,7 @@
             pair_d[own, span(width // TILE + j, TILE)] = (grad * act_all[own, cols]).astype(BF16)
             return total
 
-        total = lax.fori_loop(0, width // TILE, tile, jnp.zeros((rows, 1), F32))
+        total = lax.fori_loop(0, width // TILE, tile, jnp.zeros((rows, 1), F32), unroll=True)
         comb_out[b] = jnp.broadcast_to(total, (rows, 128)).T[:8]
 
     def input_tile(b, j):
@@ -682,10 +680,15 @@
     else:
         total_rows(others)
 
-    picked = jnp.where(ids[...] == me.astype(F32), comb_out[me, 0:1, :], 0.0)
-    for b in others:
-        picked = picked + jnp.where(ids[...] == b.astype(F32), comb_got[b, 0:1, :], 0.0)
-    comb_grad[...] = picked
+    for k in range(top):
+
+        def pick(b, line):
+            return jnp.where(routes[0, k, pl.ds(b, 1), :] > 0.5, line, 0.0)
+
+        picked = pick(me, comb_out[me, 0:1, :])
+        for b in others:
+            picked = picked + pick(b, comb_got[b, 0:1, :])
+        comb_grad[k : k + 1, :] = picked
 
     if fold:
 
@@ -814,7 +817,10 @@
         scratch += [pltpu.SemaphoreType.DMA((count,)), pltpu.SemaphoreType.DMA((count, bits))]
     scratch += [pltpu.SemaphoreType.DMA((2,))] * 2
     scratch += [pltpu.SemaphoreType.DMA((1,))] * 2
-    routes = jnp.concatenate([expert_ids.T.astype(F32), combine.T])
+    names = lax.broadcasted_iota(jnp.int32, (2, top, table, rows), 2)
+    kind = lax.broadcasted_iota(jnp.int32, (2, top, table, rows), 0)
+    value = jnp.where(kind == 0, 1.0, combine.T[None, :, None, :])
+    routes = jnp.where(names == expert_ids.T[None, :, None, :], value, 0.0)
     input_grad, combine_grad, both, down = pl.pallas_call(
         functools.partial(layer_kernel, n, bits),
         out_shape=outs,

time: 112 us -> 111 us (level)
  no operation moved by 1% of the time
where the time goes in v6:
time: 111 us
  Pallas kernels  108 us (97%)
  other arithmetic  2.07 us (2%)
    pallas_call x1, Pallas kernels, shards(): pl.pallas_call(functools.partial(layer_kernel, n, bits), out_shape=outs,...  107 us

profile of v6, /device:TPU:0, one launch (start us, length us, event | category | flops | bytes accessed | tf_op | source)
XLA Modules:
  0.0 110.6 jit_solution(13766822471033306057)
XLA Ops:
  0.6 0.8 select_select_fusion.refs_0_
  1.4 1.3 %pad_maximum_fusion.refs_1_ = bf16[2,128,2048]{2,1,0:T(8,128)(2,1)S(1)} fusion(bf16[1,128,2048]{2,1,0:T(8,128)(2,1)} %bitcast.5, bf16[1,128,2048]{2,1,0:T(8,128)(2,1)} %bitcast.6), kind=kLoop, calls=%fused_computation | loop fusion | flops 524288 | bytes 2097152 | tf_op jit(solution)/shard_map/stack | solution.py:834
  2.7 106.6 %layer.1 = (bf16[128,2048]{1,0:T(8,128)(2,1)S(1)}, f32[2,128]{1,0:T(2,128)S(1)}, bf16[256,1536]{1,0:T(8,128)(2,1)S(1)}, bf16[96,2048]{1,0:T(8,128)(2,1)S(1)}) custom-call(f32[2,2,8,128]{3,2,1,0:T(8,128)S(1)} %select_select_fusion.refs_0_, bf16[2,128,2048]{2,1,0:T(8,128)(2,1)S(1)} %pad_maximum_fusion.refs_1_, bf16[1,2048,768]{2,1,0:T(8,128)(2,1)} %refs_2_.1, ...), custom_call_target="tpu_custom_call" | custom-call | tf_op jit(solution)/shard_map/layer/pallas_call | solution.py:824
  109.4 1.2 %deliver.1 = (bf16[128,2048]{1,0:T(8,128)(2,1)}, f32[2,128]{1,0:T(2,128)}, bf16[1,256,768]{2,1,0:T(8,128)(2,1)}, bf16[1,256,768]{2,1,0:T(8,128)(2,1)}, bf16[1,96,2048]{2,1,0:T(8,128)(2,1)}) custom-call(bf16[128,2048]{1,0:T(8,128)(2,1)S(1)} %get-tuple-element.14.rows, f32[2,128]{1,0:T(2,128)S(1)} %get-tuple-element.15.comb, ...), custom_call_target="tpu_custom_call" | custom-call | tf_op jit(solution)/shard_map/deliver/pallas_call | solution.py:754
  (1 shorter events, 0.0 us)

commit v7 on v6

--- a/solution.py
+++ b/solution.py
@@ -81,8 +81,6 @@
             )
         )
     ]
-    for item in loads:
-        item.start()
     barrier = pltpu.get_barrier_semaphore()
     for k in range(1, n):
         pl.semaphore_signal(
@@ -90,6 +88,8 @@
         )
     for b in range(bits):
         pl.semaphore_signal(barrier, inc=1, device_id={"dp": mate[b]}, device_id_type=MESH)
+    for item in loads:
+        item.start()
 
     weight = routes[1, 0]
     for k in range(1, top):
@@ -416,7 +416,7 @@
         return remote(
             part.at[c, pick, pl.ds(start, count)],
             got[i].at[c, pick],
-            send.at[c],
+            send.at[0 if kind == "both" else c],
             recv.at[c, i],
             "dp",
             mate[b],
@@ -425,14 +425,14 @@
     def staged(kind, c):
         part, _, send, recv = kinds[kind]
         slot = part.at[c, :, pl.ds(0, replicas - 1)]
-        return remote(slot, slot, send.at[c], recv.at[c, 0], "dp", rank)
+        return remote(slot, slot, send.at[0 if kind == "both" else c], recv.at[0, 0], "dp", rank)
 
     def combine(kind, c, i):
         part, got, _, _ = kinds[kind]
         count = replicas >> (i + 1)
         recv = kinds[kind][3]
         slot = got[i].at[c]
-        remote(slot, slot, kinds[kind][2].at[c], recv.at[c, i], "dp", rank).wait_recv()
+        remote(slot, slot, kinds[kind][2].at[0], recv.at[c, i], "dp", rank).wait_recv()
         for way in range(2):
             start = base(way, i + 1)
             if i == bits - 1:
@@ -457,7 +457,7 @@
                 total = part[c, way, start + k].astype(F32) + got[i][c, way, k].astype(F32)
                 part[c, way, start + k] = total.astype(BF16)
 
-            loop(0, count, add)
+            loop(0, count, add, unroll=min(count, 4))
             stage(kind, c, way, i + 1).start()
 
     def spread(kind, c, who, value):
@@ -718,11 +718,8 @@
 
     loop(0, own_down, lambda q: staged("down", q).wait_send())
 
-    def finish(c):
-        combine("both", c, bits - 1)
-        staged("both", c).wait_send()
-
-    loop(0, chunks, finish)
+    loop(0, chunks, lambda c: combine("both", c, bits - 1))
+    staged("both", slice(None)).wait_send()
 
 
 def deliver_kernel(rows, comb, both, down, *refs):
@@ -813,8 +810,8 @@
     scratch += [pltpu.SemaphoreType.DMA((3,))]
     for shape in ((2, n - 1), (1 + PIECES, n), (1,), (n,), (n,), (n,), (1,), (1,)):
         scratch.append(pltpu.SemaphoreType.DMA(shape))
-    for count in (chunks, PIECES + 1):
-        scratch += [pltpu.SemaphoreType.DMA((count,)), pltpu.SemaphoreType.DMA((count, bits))]
+    for one, count in ((1, chunks), (PIECES + 1, PIECES + 1)):
+        scratch += [pltpu.SemaphoreType.DMA((one,)), pltpu.SemaphoreType.DMA((count, bits))]
     scratch += [pltpu.SemaphoreType.DMA((2,))] * 2
     scratch += [pltpu.SemaphoreType.DMA((1,))] * 2
     names = lax.broadcasted_iota(jnp.int32, (2, top, table, rows), 2)

time: 111 us -> 111 us (level)
  no operation moved by 1% of the time
where the time goes in v7:
time: 111 us
  Pallas kernels  108 us (97%)
  other arithmetic  2.07 us (2%)
    pallas_call x1, Pallas kernels, shards(): pl.pallas_call(functools.partial(layer_kernel, n, bits), out_shape=outs,...  107 us

profile of v7, /device:TPU:0, one launch (start us, length us, event | category | flops | bytes accessed | tf_op | source)
XLA Modules:
  0.0 110.5 jit_solution(5947289497076682638)
XLA Ops:
  0.6 0.8 select_select_fusion.refs_0_
  1.4 1.3 %pad_maximum_fusion.refs_1_ = bf16[2,128,2048]{2,1,0:T(8,128)(2,1)S(1)} fusion(bf16[1,128,2048]{2,1,0:T(8,128)(2,1)} %bitcast.5, bf16[1,128,2048]{2,1,0:T(8,128)(2,1)} %bitcast.6), kind=kLoop, calls=%fused_computation | loop fusion | flops 524288 | bytes 2097152 | tf_op jit(solution)/shard_map/stack | solution.py:831
  2.7 106.6 %layer.1 = (bf16[128,2048]{1,0:T(8,128)(2,1)S(1)}, f32[2,128]{1,0:T(2,128)S(1)}, bf16[256,1536]{1,0:T(8,128)(2,1)S(1)}, bf16[96,2048]{1,0:T(8,128)(2,1)S(1)}) custom-call(f32[2,2,8,128]{3,2,1,0:T(8,128)S(1)} %select_select_fusion.refs_0_, bf16[2,128,2048]{2,1,0:T(8,128)(2,1)S(1)} %pad_maximum_fusion.refs_1_, bf16[1,2048,768]{2,1,0:T(8,128)(2,1)} %refs_2_.1, ...), custom_call_target="tpu_custom_call" | custom-call | tf_op jit(solution)/shard_map/layer/pallas_call | solution.py:821
  109.3 1.2 %deliver.1 = (bf16[128,2048]{1,0:T(8,128)(2,1)}, f32[2,128]{1,0:T(2,128)}, bf16[1,256,768]{2,1,0:T(8,128)(2,1)}, bf16[1,256,768]{2,1,0:T(8,128)(2,1)}, bf16[1,96,2048]{2,1,0:T(8,128)(2,1)}) custom-call(bf16[128,2048]{1,0:T(8,128)(2,1)S(1)} %get-tuple-element.14.rows, f32[2,128]{1,0:T(2,128)S(1)} %get-tuple-element.15.comb, ...), custom_call_target="tpu_custom_call" | custom-call | tf_op jit(solution)/shard_map/deliver/pallas_call | solution.py:751
  (1 shorter events, 0.0 us)
